TPU v7x, 32 devices: a whole 2x2x4 slice. The times are simulated.
32 devices in a mesh: dp: 2 (over x), pool: 4 (over z), ep: 4 (over y, core).
Axes of the slice: x: 2, y: 2, z: 4, core: 2. Of those that a mesh axis runs over, the one named last changes fastest.
Arguments:
- hidden: bfloat16 [2048, 1536], P(('dp', 'ep')), parts along dimension 0
- k_cache: bfloat16 [2, 2048, 128, 2, 128], P(None, ('dp', 'ep')), parts along dimension 1
- v_cache: bfloat16 [2, 2048, 128, 2, 128], P(None, ('dp', 'ep')), parts along dimension 1
- lengths: int32 [2048], P(('dp', 'ep')), parts along dimension 0
- expert_ids: int32 [2, 2048, 2], P(None, ('dp', 'ep')), parts along dimension 1
- w_query: bfloat16 [2, 1536, 1536], replicated
- w_key: bfloat16 [2, 1536, 256], replicated
- w_value: bfloat16 [2, 1536, 256], replicated
- w_out: bfloat16 [2, 1536, 1536], replicated
- w_router: float32 [2, 1536, 8], replicated
- w_gate: bfloat16 [2, 8, 1536, 4096], P(None, 'ep')
- w_up: bfloat16 [2, 8, 1536, 4096], P(None, 'ep')
- w_down: bfloat16 [2, 8, 4096, 1536], P(None, 'ep')
Outputs:
- output: bfloat16 [2048, 1536], P(('dp', 'ep')), parts along dimension 0
There are 2 independent parts. A program takes and returns all parts, laid end to end along the dimension named above; an argument that names none is the same for every part.
All inputs are finite; a program needn't handle non-finite values.
Results may differ from a plain program's by a relative error of at most 0.0190241.
Values are sent between devices in bfloat16 or wider.
A program may use at most 1 GiB of HBM per device.

v0:
```python
import jax
import jax.numpy as jnp
from jax import lax
from jax.sharding import PartitionSpec as P

EPSILON = 1e-6
ROPE_BASE = 10000.0


def rms_normed(values):
    return values * lax.rsqrt(jnp.mean(values * values, axis=-1, keepdims=True) + EPSILON)


def rotary(vectors, positions):
    half = vectors.shape[-1] // 2
    freqs = ROPE_BASE ** (-2.0 * jnp.arange(half, dtype=jnp.float32) / vectors.shape[-1])
    angle = positions[:, None, None] * freqs[None, None, :]
    cosine = jnp.cos(angle)
    sine = jnp.sin(angle)
    first = vectors[..., :half]
    second = vectors[..., half:]
    return jnp.concatenate([first * cosine - second * sine, second * cosine + first * sine], axis=-1)


def attend(hidden_blk, keys_blk, vals_blk, lens_blk, w_q, w_k, w_v, w_o):
    tok_count = hidden_blk.shape[0]
    seq_len, kv_heads, head_dim = keys_blk.shape[1], keys_blk.shape[2], keys_blk.shape[3]
    heads = w_q.shape[1] // head_dim
    group = heads // kv_heads
    hidden_f = hidden_blk.astype(jnp.float32)
    normed = rms_normed(hidden_f).astype(jnp.bfloat16)
    positions = lens_blk.astype(jnp.float32)
    query = rotary(jnp.dot(normed, w_q, preferred_element_type=jnp.float32).reshape(tok_count, heads, head_dim), positions)
    query = query.astype(jnp.bfloat16).reshape(tok_count, kv_heads, group, head_dim)
    key_new = rotary(jnp.dot(normed, w_k, preferred_element_type=jnp.float32).reshape(tok_count, kv_heads, head_dim), positions).astype(jnp.bfloat16)
    val_new = jnp.dot(normed, w_v, preferred_element_type=jnp.float32).astype(jnp.bfloat16).reshape(tok_count, kv_heads, head_dim)
    scale = head_dim ** -0.5
    scores = jnp.einsum("tkgd,tskd->tkgs", query, keys_blk, preferred_element_type=jnp.float32) * scale
    valid = jnp.arange(seq_len)[None, None, None, :] < lens_blk[:, None, None, None]
    scores = jnp.where(valid, scores, -jnp.inf)
    score_new = jnp.einsum("tkgd,tkd->tkg", query, key_new, preferred_element_type=jnp.float32) * scale
    peak = jnp.maximum(jnp.max(scores, axis=-1), score_new)
    weights = jnp.exp(scores - peak[..., None])
    weight_new = jnp.exp(score_new - peak)
    denominator = jnp.sum(weights, axis=-1) + weight_new
    mixed = jnp.einsum("tkgs,tskd->tkgd", weights.astype(jnp.bfloat16), vals_blk, preferred_element_type=jnp.float32)
    mixed = mixed + weight_new.astype(jnp.bfloat16).astype(jnp.float32)[..., None] * val_new.astype(jnp.float32)[:, :, None, :]
    attended = (mixed / denominator[..., None]).astype(jnp.bfloat16).reshape(tok_count, heads * head_dim)
    return (hidden_f + jnp.dot(attended, w_o, preferred_element_type=jnp.float32)).astype(jnp.bfloat16)


def skip_attend(hidden_blk, *rest):
    return jnp.zeros_like(hidden_blk)


def route(attn_out, ids_blk, w_r, n_experts, cap):
    mixed_in = rms_normed(attn_out.astype(jnp.float32)).astype(jnp.bfloat16)
    logits = jnp.dot(mixed_in.astype(jnp.float32), w_r, precision=lax.Precision.HIGHEST)
    gates = jax.nn.softmax(jnp.take_along_axis(logits, ids_blk, axis=1), axis=-1)
    flat_ids = ids_blk.reshape(-1)
    onehot = (flat_ids[:, None] == jnp.arange(n_experts)[None, :]).astype(jnp.int32)
    slot = jnp.sum(jnp.cumsum(onehot, axis=0) * onehot, axis=1) - 1
    target = (flat_ids * cap + slot).reshape(ids_blk.shape)
    placing = jnp.any(jnp.arange(n_experts * cap)[:, None, None] == target[None, :, :], axis=2).astype(jnp.bfloat16)
    outbound = jnp.dot(placing, mixed_in, preferred_element_type=jnp.float32).astype(jnp.bfloat16)
    return gates, target, outbound


def experts_apply(tokens, w_one, w_three, w_two):
    up_one = jnp.einsum("snci,nif->sncf", tokens, w_one, preferred_element_type=jnp.float32)
    up_three = jnp.einsum("snci,nif->sncf", tokens, w_three, preferred_element_type=jnp.float32)
    inner = (jax.nn.silu(up_one) * up_three).astype(jnp.bfloat16)
    return jnp.einsum("sncf,nfi->snci", inner, w_two, preferred_element_type=jnp.float32).astype(jnp.bfloat16)


def skip_experts(tokens, *rest):
    return jnp.zeros_like(tokens)


def combine(attn_out, gates, target, returned):
    rows = jnp.take(returned, target.reshape(-1), axis=0).reshape(target.shape[0], target.shape[1], returned.shape[1])
    mixed_sum = jnp.sum(gates[:, :, None] * rows.astype(jnp.float32), axis=1)
    return (attn_out.astype(jnp.float32) + mixed_sum).astype(jnp.bfloat16)


def solution(mesh):
    pool_size = mesh.shape["pool"]
    ep_size = mesh.shape["ep"]
    half = pool_size // 2
    n_att = half * ep_size

    def body(hidden, k_cache, v_cache, lengths, expert_ids, w_query, w_key, w_value, w_out, w_router, w_gate, w_up, w_down):
        row = lax.axis_index("pool")
        is_att = row < half
        sub = row % half
        tok_count = hidden.shape[0] // half
        model = hidden.shape[1]
        n_experts = w_router.shape[2]
        topk = expert_ids.shape[2]
        n_local = w_gate.shape[1] // half
        cap = max(2, (3 * tok_count * topk) // n_experts)
        start = sub * tok_count
        state = lax.dynamic_slice_in_dim(hidden, start, tok_count, 0)
        lens_blk = lax.dynamic_slice_in_dim(lengths, start, tok_count, 0)
        for layer in range(k_cache.shape[0]):
            keys_blk = lax.dynamic_slice_in_dim(k_cache[layer], start, tok_count, 0)
            vals_blk = lax.dynamic_slice_in_dim(v_cache[layer], start, tok_count, 0)
            ids_blk = lax.dynamic_slice_in_dim(expert_ids[layer], start, tok_count, 0)
            attended = lax.cond(is_att, attend, skip_attend, state, keys_blk, vals_blk, lens_blk, w_query[layer], w_key[layer], w_value[layer], w_out[layer])
            gates, target, outbound = route(attended, ids_blk, w_router[layer], n_experts, cap)
            grid = outbound.reshape(ep_size, half, n_local, cap, model).transpose(1, 0, 2, 3, 4)
            dispatch_buf = jnp.concatenate([jnp.zeros_like(grid), grid], axis=0).reshape(pool_size * ep_size, n_local, cap, model)
            arrived = lax.all_to_all(dispatch_buf, ("pool", "ep"), 0, 0, tiled=True)
            w_one = lax.dynamic_slice_in_dim(w_gate[layer], sub * n_local, n_local, 0)
            w_three = lax.dynamic_slice_in_dim(w_up[layer], sub * n_local, n_local, 0)
            w_two = lax.dynamic_slice_in_dim(w_down[layer], sub * n_local, n_local, 0)
            produced = lax.cond(is_att, skip_experts, experts_apply, arrived[:n_att], w_one, w_three, w_two)
            return_buf = jnp.concatenate([produced, jnp.zeros_like(produced)], axis=0)
            came_back = lax.all_to_all(return_buf, ("pool", "ep"), 0, 0, tiled=True)
            returned = came_back[n_att:].reshape(half, ep_size, n_local, cap, model).transpose(1, 0, 2, 3, 4).reshape(n_experts * cap, model)
            state = combine(attended, gates, target, returned)
        gathered = lax.all_gather(state, "pool", axis=0, tiled=True)
        return gathered[: half * tok_count]

    rows_spec = ("dp", "ep")
    in_specs = (P(rows_spec, None), P(None, rows_spec), P(None, rows_spec), P(rows_spec), P(None, rows_spec, None), P(), P(), P(), P(), P(), P(None, "ep"), P(None, "ep"), P(None, "ep"))
    return jax.shard_map(body, mesh=mesh, in_specs=in_specs, out_specs=P(rows_spec, None), check_vma=False)
```

profile of v0, /device:TPU:0, one launch (start us, length us, event | category | flops | bytes accessed | tf_op | source)
XLA Modules:
  0.0 985.6 jit_solution(5311791791197162515)
XLA Ops:
  11.4 121.1 %conditional.4 = (f32[128,1536]{1,0:T(8,128)S(1)}, f32[128,1]{0,1:T(1,128)S(1)}) conditional(s32[]{:T(128)} %convert_element_type.228, () %tuple.56, (bf16[256,1536]{1,0:T(8,128)(2,1)}, s32[]{:T(128)}, s32[128]{0:T(128)}, bf16[2,1536,1536]{2,1,0:T(8,128)(2,1)}, bf16[2,256,128,2,128]{4,3,2,1,0:T(2,128)(2,1)}, ...), branch_computations={%region_0.1_spmd, %region_1.6_spmd} | conditional | flops 1518765312 | bytes 294324928 | solution.py:109
  11.5 22.9 %copy.120 = bf16[2,256,128,2,128]{4,2,3,1,0:T(8,128)(2,1)} copy(bf16[2,256,128,2,128]{4,3,2,1,0:T(2,128)(2,1)} %get-tuple-element.384) | data formatting | bytes 67108864 | tf_op jit(solution)/shard_map
  34.3 14.1 %slice.219 = bf16[1,256,128,2,128]{4,2,3,1,0:T(8,128)(2,1)} slice(bf16[2,256,128,2,128]{4,2,3,1,0:T(8,128)(2,1)} %copy.120), slice={[0:1], [0:256], [0:128], [0:2], [0:128]} | slice | bytes 33554432 | tf_op jit(solution)/shard_map/slice | solution.py:107
  48.4 22.9 %copy.118 = bf16[2,256,128,2,128]{4,2,3,1,0:T(8,128)(2,1)} copy(bf16[2,256,128,2,128]{4,3,2,1,0:T(2,128)(2,1)} %get-tuple-element.382) | data formatting | bytes 67108864 | tf_op jit(solution)/shard_map
  71.3 14.1 %slice.215 = bf16[1,256,128,2,128]{4,2,3,1,0:T(8,128)(2,1)} slice(bf16[2,256,128,2,128]{4,2,3,1,0:T(8,128)(2,1)} %copy.118), slice={[0:1], [0:256], [0:128], [0:2], [0:128]} | slice | bytes 33554432 | tf_op jit(solution)/shard_map/slice | solution.py:106
  85.4 12.7 %copy.117 = bf16[2,1536,1536]{1,2,0:T(8,128)(2,1)} copy(bf16[2,1536,1536]{2,1,0:T(8,128)(2,1)} %get-tuple-element.381) | data formatting | bytes 18874368 | tf_op jit(solution)/shard_map
  104.7 8.9 fusion.202
  113.7 1.8 copy.119
  119.0 1.9 fusion.34
  121.1 1.6 fusion.27
  122.8 5.8 fusion.31
  129.0 3.3 multiply_reduce_fusion
  133.6 2.5 concatenate.46.clone
  136.1 5.4 all-to-all-start
  141.6 86.9 %all-to-all-done = bf16[16,1,96,1536]{3,2,1,0:T(8,128)(2,1)} async-done(((bf16[16,1,96,1536]{3,2,1,0:T(8,128)(2,1)}), bf16[16,1,96,1536]{3,2,1,0:T(8,128)(2,1)}, u32[]{:S(2)}, u32[]{:S(2)}) %all-to-all-start) | async-done | bytes 4718624 | tf_op jit(solution)/shard_map/all_to_all | solution.py:113
  228.7 2.6 concatenate.47
  231.3 127.3 %all-to-all-start.1 = ((bf16[16,1,96,1536]{3,2,1,0:T(8,128)(2,1)}), bf16[16,1,96,1536]{3,2,1,0:T(8,128)(2,1)}, u32[]{:S(2)}, u32[]{:S(2)}) async-start(bf16[16,1,96,1536]{3,2,1,0:T(8,128)(2,1)} %concatenate.47), calls=%async_computation.1 | async-start | bytes 9437184 | tf_op jit(solution)/shard_map/all_to_all | solution.py:119
  363.5 81.7 %all-to-all-done.1 = bf16[16,1,96,1536]{3,2,1,0:T(8,128)(2,1)} async-done(((bf16[16,1,96,1536]{3,2,1,0:T(8,128)(2,1)}), bf16[16,1,96,1536]{3,2,1,0:T(8,128)(2,1)}, u32[]{:S(2)}, u32[]{:S(2)}) %all-to-all-start.1) | async-done | bytes 4718624 | tf_op jit(solution)/shard_map/all_to_all | solution.py:119
  445.2 1.8 slice.231
  447.2 2.1 gather_fusion.1
  449.3 2.6 select_convert_fusion.1
  451.9 3.0 reshape.512
  454.9 3.6 multiply_reduce_fusion.3
  458.7 122.1 %conditional.6 = (f32[128,1536]{1,0:T(8,128)S(1)}, f32[128,1]{0,1:T(1,128)S(1)}) conditional(s32[]{:T(128)} %convert_element_type.228, () %tuple.55, (bf16[128,1536]{1,0:T(8,128)(2,1)S(1)}, s32[128]{0:T(128)}, bf16[2,1536,1536]{2,1,0:T(8,128)(2,1)}, bf16[2,256,128,2,128]{4,3,2,1,0:T(2,128)(2,1)}, s32[]{:T(128)}, ...), branch_computations={%region_15.18_spmd, %region_16.23_spmd} | conditional | flops 1518765312 | bytes 282002560 | solution.py:109
  458.9 22.9 %copy.134 = bf16[2,256,128,2,128]{4,2,3,1,0:T(8,128)(2,1)} copy(bf16[2,256,128,2,128]{4,3,2,1,0:T(2,128)(2,1)} %get-tuple-element.398) | data formatting | bytes 67108864 | tf_op jit(solution)/shard_map
  481.7 14.1 %slice.228 = bf16[1,256,128,2,128]{4,2,3,1,0:T(8,128)(2,1)} slice(bf16[2,256,128,2,128]{4,2,3,1,0:T(8,128)(2,1)} %copy.134), slice={[1:2], [0:256], [0:128], [0:2], [0:128]} | slice | bytes 33554432 | tf_op jit(solution)/shard_map/slice | solution.py:107
  495.8 22.9 %copy.132 = bf16[2,256,128,2,128]{4,2,3,1,0:T(8,128)(2,1)} copy(bf16[2,256,128,2,128]{4,3,2,1,0:T(2,128)(2,1)} %get-tuple-element.395) | data formatting | bytes 67108864 | tf_op jit(solution)/shard_map
  518.7 14.1 %slice.224 = bf16[1,256,128,2,128]{4,2,3,1,0:T(8,128)(2,1)} slice(bf16[2,256,128,2,128]{4,2,3,1,0:T(8,128)(2,1)} %copy.132), slice={[1:2], [0:256], [0:128], [0:2], [0:128]} | slice | bytes 33554432 | tf_op jit(solution)/shard_map/slice | solution.py:106
  532.8 12.7 %copy.131 = bf16[2,1536,1536]{1,2,0:T(8,128)(2,1)} copy(bf16[2,1536,1536]{2,1,0:T(8,128)(2,1)} %get-tuple-element.394) | data formatting | bytes 18874368 | tf_op jit(solution)/shard_map
  545.6 2.2 slice-done.1
  553.5 8.9 fusion.203
  562.4 1.8 copy.133
  567.5 1.9 fusion.126
  571.2 5.7 fusion.123
  577.3 3.2 multiply_reduce_fusion.1
  580.8 1.8 convolution_convert_fusion.2
  582.8 2.5 concatenate.48.clone
  585.4 21.0 %all-to-all-start.2 = ((bf16[16,1,96,1536]{3,2,1,0:T(8,128)(2,1)}), bf16[16,1,96,1536]{3,2,1,0:T(8,128)(2,1)}, u32[]{:S(2)}, u32[]{:S(2)}) async-start(bf16[16,1,96,1536]{3,2,1,0:T(8,128)(2,1)} %bitcast.349), calls=%async_computation.2 | async-start | bytes 9437184 | tf_op jit(solution)/shard_map/all_to_all | solution.py:113
  606.3 86.9 %all-to-all-done.2 = bf16[16,1,96,1536]{3,2,1,0:T(8,128)(2,1)} async-done(((bf16[16,1,96,1536]{3,2,1,0:T(8,128)(2,1)}), bf16[16,1,96,1536]{3,2,1,0:T(8,128)(2,1)}, u32[]{:S(2)}, u32[]{:S(2)}) %all-to-all-start.2) | async-done | bytes 4718624 | tf_op jit(solution)/shard_map/all_to_all | solution.py:113
  693.5 2.6 concatenate.49
  696.0 126.8 %all-to-all-start.3 = ((bf16[16,1,96,1536]{3,2,1,0:T(8,128)(2,1)}), bf16[16,1,96,1536]{3,2,1,0:T(8,128)(2,1)}, u32[]{:S(2)}, u32[]{:S(2)}) async-start(bf16[16,1,96,1536]{3,2,1,0:T(8,128)(2,1)} %concatenate.49), calls=%async_computation.3 | async-start | bytes 9437184 | tf_op jit(solution)/shard_map/all_to_all | solution.py:119
  825.8 83.9 %all-to-all-done.3 = bf16[16,1,96,1536]{3,2,1,0:T(8,128)(2,1)} async-done(((bf16[16,1,96,1536]{3,2,1,0:T(8,128)(2,1)}), bf16[16,1,96,1536]{3,2,1,0:T(8,128)(2,1)}, u32[]{:S(2)}, u32[]{:S(2)}) %all-to-all-start.3) | async-done | bytes 4718624 | tf_op jit(solution)/shard_map/all_to_all | solution.py:119
  909.7 1.8 slice.233
  911.7 2.1 gather_fusion.3
  915.2 2.1 reshape.513
  917.3 3.6 multiply_reduce_fusion.2
  921.8 54.4 %all-gather.2.cloned.1.call-done = bf16[512,1536]{1,0:T(8,128)(2,1)} async-done(((bf16[128,1536]{1,0:T(8,128)(2,1)}), bf16[512,1536]{1,0:T(8,128)(2,1)}) %all-gather.2.cloned.1.call-update) | async-done | bytes 1572880 | tf_op jit(solution)/shard_map/all_gather | solution.py:122
  976.2 2.1 slice.234
  (179 shorter events, 38.9 us)
Async XLA Ops:
  7.8 1.7 copy-start.16
  8.2 2.3 copy-start.20
  10.5 0.6 copy-start.22
  98.1 1.1 copy-start.8
  98.1 2.6 slice-start
  100.6 13.0 %copy-start.5 = (bf16[2,1536,256]{2,1,0:T(8,128)(2,1)S(1)}, bf16[2,1536,256]{2,1,0:T(8,128)(2,1)}, u32[]{:S(2)}) copy-start(bf16[2,1536,256]{2,1,0:T(8,128)(2,1)} %get-tuple-element.383) | copy-start | bytes 4718596 | tf_op jit(solution)/shard_map/cond
  115.4 7.3 copy-start.6
  122.8 6.2 copy-start.9
  132.5 3.6 copy-start
  132.6 3.5 copy-start.30
  136.1 92.3 %all-to-all-start = ((bf16[16,1,96,1536]{3,2,1,0:T(8,128)(2,1)}), bf16[16,1,96,1536]{3,2,1,0:T(8,128)(2,1)}, u32[]{:S(2)}, u32[]{:S(2)}) async-start(bf16[16,1,96,1536]{3,2,1,0:T(8,128)(2,1)} %bitcast.348), calls=%async_computation | async-start | bytes 9437184 | tf_op jit(solution)/shard_map/all_to_all | solution.py:113
  228.6 129.9 %copy-start.14 = (s32[1,128,2]{1,2,0:T(2,128)S(1)}, s32[1,128,2]{1,2,0:T(2,128)}, u32[]{:S(2)}) copy-start(s32[1,128,2]{1,2,0:T(2,128)} %get-tuple-element.409) | copy-start | bytes 3076
  228.6 130.3 %copy-start.27 = (s32[128,2,1]{0,1,2:T(2,128)S(1)}, s32[128,2,1]{0,1,2:T(2,128)}, u32[]{:S(2)}) copy-start(s32[128,2,1]{0,1,2:T(2,128)} %get-tuple-element.444) | copy-start | bytes 3076
  228.7 130.6 %copy-start.1 = (f32[128,1536]{1,0:T(8,128)S(1)}, f32[128,1536]{1,0:T(8,128)}, u32[]{:S(2)}) copy-start(f32[128,1536]{1,0:T(8,128)} %copy-done) | copy-start | bytes 2359300
  228.7 130.6 %copy-start.12 = (f32[2,1536,8]{1,2,0:T(8,128)S(1)}, f32[2,1536,8]{1,2,0:T(8,128)}, u32[]{:S(2)}) copy-start(f32[2,1536,8]{1,2,0:T(8,128)} %param.34) | copy-start | bytes 294916
  228.7 130.6 %copy-start.31 = (f32[128]{0:T(128)S(1)}, f32[128]{0:T(128)}, u32[]{:S(2)}) copy-start(f32[128]{0:T(128)} %copy-done.30) | copy-start | bytes 1540
  231.3 213.9 %all-to-all-start.1 = ((bf16[16,1,96,1536]{3,2,1,0:T(8,128)(2,1)}), bf16[16,1,96,1536]{3,2,1,0:T(8,128)(2,1)}, u32[]{:S(2)}, u32[]{:S(2)}) async-start(bf16[16,1,96,1536]{3,2,1,0:T(8,128)(2,1)} %concatenate.47), calls=%async_computation.1 | async-start | bytes 9437184 | tf_op jit(solution)/shard_map/all_to_all | solution.py:119
  359.0 3.4 copy-start.18
  359.7 1.6 copy-start.17
  359.7 3.0 copy-start.21
  359.7 3.0 copy-start.23
  362.5 84.5 %copy-start.24 = (s32[256]{0:T(256)}, s32[256]{0:T(256)S(1)}, u32[]{:S(2)}) copy-start(s32[256]{0:T(256)S(1)} %fusion.192) | copy-start | bytes 3076
  449.3 9.4 copy-start.4
  545.5 2.3 slice-start.1
  550.1 12.3 %copy-start.10 = (f32[128,64]{0,1:T(8,128)}, f32[128,64]{0,1:T(8,128)S(1)}, u32[]{:S(2)}) copy-start(f32[128,64]{0,1:T(8,128)S(1)} %get-tuple-element.436) | copy-start | bytes 98308 | tf_op jit(solution)/shard_map/cond
  550.2 12.3 %copy-start.11 = (f32[128,64]{0,1:T(8,128)}, f32[128,64]{0,1:T(8,128)S(1)}, u32[]{:S(2)}) copy-start(f32[128,64]{0,1:T(8,128)S(1)} %get-tuple-element.437) | copy-start | bytes 98308 | tf_op jit(solution)/shard_map/cond
  564.2 6.9 copy-start.7
  580.8 4.6 copy-start.2
  580.8 1.9 copy-start.28
  585.4 107.8 %all-to-all-start.2 = ((bf16[16,1,96,1536]{3,2,1,0:T(8,128)(2,1)}), bf16[16,1,96,1536]{3,2,1,0:T(8,128)(2,1)}, u32[]{:S(2)}, u32[]{:S(2)}) async-start(bf16[16,1,96,1536]{3,2,1,0:T(8,128)(2,1)} %bitcast.349), calls=%async_computation.2 | async-start | bytes 9437184 | tf_op jit(solution)/shard_map/all_to_all | solution.py:113
  693.4 129.8 %copy-start.26 = (s32[128,2,1]{0,1,2:T(2,128)S(1)}, s32[128,2,1]{0,1,2:T(2,128)}, u32[]{:S(2)}) copy-start(s32[128,2,1]{0,1,2:T(2,128)} %get-tuple-element.408) | copy-start | bytes 3076
  693.4 130.1 %copy-start.19 = (s32[256]{0:T(256)S(1)}, s32[256]{0:T(256)}, u32[]{:S(2)}) copy-start(s32[256]{0:T(256)} %copy-done.18) | copy-start | bytes 3076
  693.4 130.1 %copy-start.25 = (s32[256]{0:T(256)S(1)}, s32[256]{0:T(256)}, u32[]{:S(2)}) copy-start(s32[256]{0:T(256)} %copy-done.24) | copy-start | bytes 3076
  693.4 130.1 %copy-start.3 = (f32[128,1536]{1,0:T(8,128)S(1)}, f32[128,1536]{1,0:T(8,128)}, u32[]{:S(2)}) copy-start(f32[128,1536]{1,0:T(8,128)} %copy-done.2) | copy-start | bytes 2359300
  693.4 130.1 %copy-start.13 = (f32[2,1536,8]{1,2,0:T(8,128)S(1)}, f32[2,1536,8]{1,2,0:T(8,128)}, u32[]{:S(2)}) copy-start(f32[2,1536,8]{1,2,0:T(8,128)} %param.34) | copy-start | bytes 294916
  693.5 130.1 %copy-start.29 = (f32[128]{0:T(128)S(1)}, f32[128]{0:T(128)}, u32[]{:S(2)}) copy-start(f32[128]{0:T(128)} %copy-done.28) | copy-start | bytes 1540
  696.0 213.7 %all-to-all-start.3 = ((bf16[16,1,96,1536]{3,2,1,0:T(8,128)(2,1)}), bf16[16,1,96,1536]{3,2,1,0:T(8,128)(2,1)}, u32[]{:S(2)}, u32[]{:S(2)}) async-start(bf16[16,1,96,1536]{3,2,1,0:T(8,128)(2,1)} %concatenate.49), calls=%async_computation.3 | async-start | bytes 9437184 | tf_op jit(solution)/shard_map/all_to_all | solution.py:119
  822.9 153.3 %all-gather.2.cloned.1.call-start = ((), (), s32[]{:S(2)}) async-start(), calls=%async_computation.4 | async-start | bytes 1966080 | tf_op jit(solution)/shard_map/all_gather | solution.py:122
  824.0 1.6 copy-start.15
Sparse Core Ops, SparseCore 0:
  921.9 54.2 all-gather.1
where the time goes:
time: 994 us; the launch traced here: 986 us
  waiting for transfers between devices  394 us (40%)
  starting transfers between devices  281 us (28%)
  local copies, waits for them, and re-layouts  222 us (22%)
  matrix products  48.4 us (5%)
  other arithmetic  24.8 us (2%)
  between operations  14.5 us (1%)
    all_to_all x2, starting transfers between devices, body(): came_back = lax.all_to_all(return_buf, ('pool', 'ep'), 0, 0, tiled=True)  254 us
    all_to_all x2, waiting for transfers between devices, body(): arrived = lax.all_to_all(dispatch_buf, ('pool', 'ep'), 0, 0, tiled=True)  174 us
    all_to_all x2, waiting for transfers between devices, body(): came_back = lax.all_to_all(return_buf, ('pool', 'ep'), 0, 0, tiled=True)  166 us
    another operation x13, local copies, waits for them, and re-layouts  121 us
    all_gather x1, waiting for transfers between devices, body(): gathered = lax.all_gather(state, 'pool', axis=0, tiled=True)  54.4 us
    slice x2, local copies, waits for them, and re-layouts, body(): vals_blk = lax.dynamic_slice_in_dim(v_cache[layer], start, tok_count, 0)  28.2 us
    slice x2, local copies, waits for them, and re-layouts, body(): keys_blk = lax.dynamic_slice_in_dim(k_cache[layer], start, tok_count, 0)  28.2 us
    all_to_all x2, starting transfers between devices, body(): arrived = lax.all_to_all(dispatch_buf, ('pool', 'ep'), 0, 0, tiled=True)  26.4 us
  transfers between devices with their start and end apart: 5, of which 5 were waited for; matrix products, arithmetic and copies ran while one was open for 1% of the time, Pallas kernels for 0%

commit v1 on v0

v1 whole, which is shorter than its diff:
```python
import functools
import math

import jax
import jax.numpy as jnp
import numpy as np
from jax import lax
from jax.experimental import pallas as pl
from jax.experimental.pallas import tpu as pltpu
from jax.sharding import PartitionSpec as P

EPSILON = 1e-6
ROPE_BASE = 10000.0
MESH = pl.DeviceIdType.MESH
HEAD = 128
KV = 2
LANES = 128
CHUNK = 512
GU_SLOTS = 5
DOWN_SLOTS = 3
KV_BLOCKS = 4
UNROLL = 4


def rotary_tables(size):
    half = HEAD // 2
    freqs = np.float32(ROPE_BASE) ** (np.float32(-2.0) * np.arange(half, dtype=np.float32) / np.float32(HEAD))
    angle = np.arange(size, dtype=np.float32)[:, None] * freqs[None, :].astype(np.float32)
    cosine = np.cos(angle).astype(np.float32)
    sine = np.sin(angle).astype(np.float32)
    return np.concatenate([cosine, cosine], 1), np.concatenate([-sine, sine], 1)


def normed(values):
    return values * lax.rsqrt(jnp.mean(values * values, axis=-1, keepdims=True) + EPSILON)


def kernel(dims, lens, ids, hid, kc, vc, wq, wk, wv, wo, wr, cos_t, sin_t, wg, wu, wd, out,
           wq_b, wkv_b, wo_b, kbuf, vbuf, gu, dbuf, ubuf, inner, stage, part_l, part_m, merged, far, xg, acc_a,
           q2d, k2d, v2d, o2d, att, gbuf, gsel, wr_b, cosb, sinb, cosr, sinr, id_b,
           wsem, kvsem, gusem, dsem, isem, us, ur, gs, gr, ps, pr, ms, mr, fs, fr, zs, zr, osem):
    layers, toks, model, ff, heads, local = dims
    e = lax.axis_index("ep")
    p = lax.axis_index("pool")
    pools = 4
    partner = e + 1 - 2 * (e % 2)
    cross = (e + 2) % 4
    start = p * toks
    ff_chunks = ff // CHUNK
    gu_total = local * ff_chunks
    d_chunks = model // CHUNK
    d_total = d_chunks * local
    rows = 4 * toks
    group = heads // KV
    seq2 = kbuf.shape[1]
    per_block = toks // KV_BLOCKS

    def remote(src, dst, ssem, rsem, axis, index):
        return pltpu.make_async_remote_copy(src_ref=src, dst_ref=dst, send_sem=ssem, recv_sem=rsem,
                                            device_id={axis: index}, device_id_type=MESH)

    def gu_copies(g):
        layer, i, slot = g // gu_total, g % gu_total, g % GU_SLOTS
        expert, c = i // ff_chunks, i % ff_chunks
        cols = pl.ds(pl.multiple_of(c * CHUNK, CHUNK), CHUNK)
        return [pltpu.make_async_copy(w.at[layer, expert, :, cols], gu.at[slot, k], gusem.at[slot, k])
                for k, w in enumerate((wg, wu))]

    def d_copy(d):
        layer, i, slot = d // d_total, d % d_total, d % DOWN_SLOTS
        j, expert = i // local, i % local
        cols = pl.ds(pl.multiple_of(j * CHUNK, CHUNK), CHUNK)
        return pltpu.make_async_copy(wd.at[layer, expert, :, cols], dbuf.at[slot], dsem.at[slot])

    kvw = KV * HEAD

    def weight_copies(layer):
        return [pltpu.make_async_copy(wq.at[layer], wq_b, wsem.at[0]),
                pltpu.make_async_copy(wk.at[layer], wkv_b.at[:, pl.ds(0, kvw)], wsem.at[1]),
                pltpu.make_async_copy(wv.at[layer], wkv_b.at[:, pl.ds(kvw, kvw)], wsem.at[2]),
                pltpu.make_async_copy(wo.at[layer], wo_b, wsem.at[3])]

    def kv_copies(layer, b):
        here = pl.ds(start + b * per_block, per_block)
        there = pl.ds(b * per_block, per_block)
        return [pltpu.make_async_copy(kc.at[layer, here], kbuf.at[there], kvsem.at[b, 0]),
                pltpu.make_async_copy(vc.at[layer, here], vbuf.at[there], kvsem.at[b, 1])]

    def start_attention(layer):
        copies = weight_copies(layer)
        for c in copies[:3]:
            c.start()
        for b in range(KV_BLOCKS):
            for c in kv_copies(layer, b):
                c.start()
        copies[3].start()

    first = [pltpu.make_async_copy(hid.at[pl.ds(start, toks)], acc_a, isem.at[0]),
             pltpu.make_async_copy(wr, wr_b, isem.at[1]),
             pltpu.make_async_copy(cos_t, cosb, isem.at[2]),
             pltpu.make_async_copy(sin_t, sinb, isem.at[3])]
    for c in first:
        c.start()
    start_attention(0)
    for g in range(GU_SLOTS):
        for c in gu_copies(g):
            c.start()
    for d in range(DOWN_SLOTS):
        d_copy(d).start()

    barrier = pltpu.get_barrier_semaphore()
    pl.semaphore_signal(barrier, inc=1, device_id={"ep": partner}, device_id_type=MESH)
    pl.semaphore_signal(barrier, inc=1, device_id={"ep": cross}, device_id_type=MESH)

    @pl.when(p > 0)
    def _():
        pl.semaphore_signal(barrier, inc=1, device_id={"pool": p - 1}, device_id_type=MESH)

    @pl.when(p < pools - 1)
    def _():
        pl.semaphore_signal(barrier, inc=1, device_id={"pool": p + 1}, device_id_type=MESH)

    middle = (p > 0) & (p < pools - 1)

    @pl.when(middle)
    def _():
        pl.semaphore_wait(barrier, 4)

    @pl.when(jnp.logical_not(middle))
    def _():
        pl.semaphore_wait(barrier, 3)

    for c in first:
        c.wait()

    zeros = jnp.zeros(((16 - heads) * toks, HEAD), jnp.float32)
    for ref in (q2d, k2d, v2d):
        ref[pl.ds(heads * toks, (16 - heads) * toks), :] = zeros

    def spread(t, carry):
        where = pl.ds(t, 1)
        n = lens[start + t]
        cosr[where, :] = cosb[pl.ds(n, 1), :]
        sinr[where, :] = sinb[pl.ds(n, 1), :]
        for layer in range(layers):
            for k in range(2):
                id_b[layer, k, where, :] = jnp.full((1, LANES), ids[layer, k, start + t], jnp.int32)
        return carry

    lax.fori_loop(0, toks, spread, 0)

    lane = lax.broadcasted_iota(jnp.int32, (16, seq2), 1)
    head_kv = jnp.where(lax.broadcasted_iota(jnp.int32, (16, seq2), 0) >= group, 1, 0)
    parity = (lane % KV) == head_kv
    scale = HEAD ** -0.5

    def layer_body(layer, carry):
        hidden = acc_a[...].astype(jnp.float32)
        h = normed(hidden).astype(jnp.bfloat16)
        copies = weight_copies(layer)
        copies[0].wait()
        cosine, sine = cosr[...], sinr[...]

        def rope(v):
            return (v * cosine + pltpu.roll(v, HEAD // 2, 1) * sine).astype(jnp.bfloat16).astype(jnp.float32)

        for n in range(heads * HEAD // CHUNK):
            qn = jnp.dot(h, wq_b[:, n * CHUNK:(n + 1) * CHUNK], preferred_element_type=jnp.float32)
            for k in range(CHUNK // HEAD):
                head = n * (CHUNK // HEAD) + k
                q2d[pl.ds(head * toks, toks), :] = rope(qn[:, k * HEAD:(k + 1) * HEAD])
        copies[1].wait()
        copies[2].wait()
        kv = jnp.dot(h, wkv_b[...], preferred_element_type=jnp.float32)
        for j in range(KV):
            kj = rope(kv[:, j * HEAD:(j + 1) * HEAD])
            vj = kv[:, kvw + j * HEAD:kvw + (j + 1) * HEAD].astype(jnp.bfloat16).astype(jnp.float32)
            for k in range(group):
                at = pl.ds((j * group + k) * toks, toks)
                k2d[at, :] = kj
                v2d[at, :] = vj

        def one_token(t):
            at = pl.ds(t, 16, stride=toks)
            q = q2d[at, :]
            n2 = lens[start + t] * KV
            s = lax.dot_general(q.astype(jnp.bfloat16), kbuf[t], (((1,), (1,)), ((), ())),
                                preferred_element_type=jnp.float32) * scale
            s = jnp.where(parity & (lane < n2), s, -jnp.inf)
            s_new = jnp.sum(q * k2d[at, :], axis=1, keepdims=True) * scale
            peak = jnp.maximum(jnp.max(s, axis=1, keepdims=True), s_new)
            w = jnp.exp(s - peak)
            w_new = jnp.exp(s_new - peak)
            total = jnp.sum(w, axis=1, keepdims=True) + w_new
            o = jnp.dot(w.astype(jnp.bfloat16), vbuf[t], preferred_element_type=jnp.float32)
            o = o + w_new.astype(jnp.bfloat16).astype(jnp.float32) * v2d[at, :]
            o2d[at, :] = o / total

        for b in range(KV_BLOCKS):
            for c in kv_copies(layer, b):
                c.wait()

            def some_tokens(i, carry, b=b):
                for k in range(UNROLL):
                    one_token(b * per_block + i * UNROLL + k)
                return carry

            lax.fori_loop(0, per_block // UNROLL, some_tokens, 0)

        for head in range(heads):
            att[:, head * HEAD:(head + 1) * HEAD] = o2d[pl.ds(head * toks, toks), :].astype(jnp.bfloat16)
        copies[3].wait()
        mean_sq = jnp.zeros((toks, 1), jnp.float32)
        for n in range(model // CHUNK):
            cols = slice(n * CHUNK, (n + 1) * CHUNK)
            a = acc_a[:, cols].astype(jnp.float32) + jnp.dot(att[...], wo_b[:, cols], preferred_element_type=jnp.float32)
            acc_a[:, cols] = a.astype(jnp.bfloat16)

        u = normed(acc_a[...].astype(jnp.float32)).astype(jnp.bfloat16)
        ubuf[layer, pl.ds(0, toks), :] = u

        def block(ref, b):
            return ref.at[layer, pl.ds(b * toks, toks)]

        u_near = remote(block(ubuf, 0), block(ubuf, 1), us.at[0], ur.at[layer, 0], "ep", partner)
        u_far = remote(block(ubuf, 0), block(ubuf, 2), us.at[1], ur.at[layer, 1], "ep", cross)
        u_pass = remote(block(ubuf, 2), block(ubuf, 3), us.at[2], ur.at[layer, 2], "ep", partner)
        g_near = remote(block(gbuf, 0), block(gbuf, 1), gs.at[0], gr.at[layer, 0], "ep", partner)
        g_far = remote(block(gbuf, 0), block(gbuf, 2), gs.at[1], gr.at[layer, 1], "ep", cross)
        g_pass = remote(block(gbuf, 2), block(gbuf, 3), gs.at[2], gr.at[layer, 2], "ep", partner)
        u_far.start()
        u_near.start()

        wl = wr_b[layer]
        hi = wl.astype(jnp.bfloat16).astype(jnp.float32)
        rest = wl - hi
        mid = rest.astype(jnp.bfloat16).astype(jnp.float32)
        low = rest - mid
        wide = jnp.concatenate([hi, mid, low, jnp.zeros((LANES - 3 * wl.shape[0], model), jnp.float32)], axis=0).astype(jnp.bfloat16)
        parts = lax.dot_general(u, wide, (((1,), (1,)), ((), ())), preferred_element_type=jnp.float32)
        logits = parts + pltpu.roll(parts, LANES - 8, 1) + pltpu.roll(parts, LANES - 16, 1)
        expert_lane = lax.broadcasted_iota(jnp.int32, (toks, LANES), 1)
        chosen = (id_b[layer, 0] == expert_lane) | (id_b[layer, 1] == expert_lane)
        logits = jnp.where(chosen, logits, -jnp.inf)
        ew = jnp.exp(logits - jnp.max(logits, axis=1, keepdims=True))
        gbuf[layer, pl.ds(0, toks), :] = ew / jnp.sum(ew, axis=1, keepdims=True)
        g_far.start()
        g_near.start()
        u_far.wait_recv()
        u_pass.start()
        g_far.wait_recv()
        g_pass.start()
        for c in (u_near, u_pass, g_near, g_pass):
            c.wait_recv()

        gates = gbuf[layer]
        row_lane = lax.broadcasted_iota(jnp.int32, (rows, LANES), 1)
        for k in range(local):
            one = jnp.sum(jnp.where(row_lane == e * local + k, gates, 0.0), axis=1, keepdims=True)
            gsel[k] = jnp.broadcast_to(one, (rows, LANES))

        def gu_body(i, carry):
            g = layer * gu_total + i
            slot = g % GU_SLOTS
            for c in gu_copies(g):
                c.wait()
            tokens = ubuf[layer]
            one = jnp.dot(tokens, gu[slot, 0], preferred_element_type=jnp.float32)
            three = jnp.dot(tokens, gu[slot, 1], preferred_element_type=jnp.float32)
            cols = pl.ds(pl.multiple_of((i % ff_chunks) * CHUNK, CHUNK), CHUNK)
            inner[i // ff_chunks, :, cols] = (jax.nn.silu(one) * three).astype(jnp.bfloat16)

            @pl.when(g + GU_SLOTS < layers * gu_total)
            def _():
                for c in gu_copies(g + GU_SLOTS):
                    c.start()

            return carry

        lax.fori_loop(0, gu_total, gu_body, 0)

        @pl.when(layer + 1 < layers)
        def _():
            start_attention(layer + 1)

        def near_copies(j):
            return [remote(stage.at[j, pl.ds(toks, toks)], part_l.at[layer, j], ps.at[j], pr.at[layer, j], "ep", partner),
                    remote(stage.at[j, pl.ds(3 * toks, toks)], part_m.at[layer, j], ms.at[j], mr.at[layer, j], "ep", partner)]

        def far_copy(j):
            return remote(merged.at[j], far.at[layer, j], fs.at[j], fr.at[layer, j], "ep", cross)

        def merge(j):
            near_copies(j)[1].wait_recv()
            merged[j] = stage[j, pl.ds(2 * toks, toks), :] + part_m[layer, j]
            far_copy(j).start()

        def d_body(j, carry):
            for k in range(local):
                d = layer * d_total + j * local + k
                slot = d % DOWN_SLOTS
                d_copy(d).wait()
                y = jnp.dot(inner[k], dbuf[slot], preferred_element_type=jnp.float32).astype(jnp.bfloat16).astype(jnp.float32)
                gate = gsel[k]
                for n in range(CHUNK // LANES):
                    cols = slice(n * LANES, (n + 1) * LANES)
                    term = jnp.where(gate > 0.0, gate * y[:, cols], 0.0)
                    if k > 0:
                        term = stage[j, :, cols] + term
                    stage[j, :, cols] = term

                @pl.when(d + DOWN_SLOTS < layers * d_total)
                def _():
                    d_copy(d + DOWN_SLOTS).start()

            for c in reversed(near_copies(j)):
                c.start()

            @pl.when(j > 0)
            def _():
                merge(j - 1)

            return carry

        lax.fori_loop(0, d_chunks, d_body, 0)
        merge(d_chunks - 1)

        for j in range(d_chunks):
            cols = slice(j * CHUNK, (j + 1) * CHUNK)
            near_copies(j)[0].wait_recv()
            far_copy(j).wait_recv()
            total = (stage[j, pl.ds(0, toks), :] + part_l[layer, j]) + far[layer, j]
            acc_a[:, cols] = (acc_a[:, cols].astype(jnp.float32) + total).astype(jnp.bfloat16)

        for c in (u_near, u_far, u_pass, g_near, g_far, g_pass):
            c.wait_send()
        for j in range(d_chunks):
            for c in near_copies(j):
                c.wait_send()
            far_copy(j).wait_send()
        return carry

    lax.fori_loop(0, layers, layer_body, 0)

    xg[p] = acc_a[...]

    def shift(origin, way):
        return remote(xg.at[origin], xg.at[origin], zs.at[way, origin], zr.at[origin], "pool", p + 1 - 2 * way)

    def store(origin):
        return pltpu.make_async_copy(xg.at[origin], out.at[pl.ds(origin * toks, toks)], osem.at[origin])

    @pl.when(p < pools - 1)
    def _():
        shift(p, 0).start()

    @pl.when(p > 0)
    def _():
        shift(p, 1).start()

    store(p).start()
    for step in range(1, pools):
        @pl.when(p - step >= 0)
        def _(step=step):
            shift(p - step, 0).wait_recv()

            @pl.when(p < pools - 1)
            def _():
                shift(p - step, 0).start()

            store(p - step).start()

        @pl.when(p + step < pools)
        def _(step=step):
            shift(p + step, 1).wait_recv()

            @pl.when(p > 0)
            def _():
                shift(p + step, 1).start()

            store(p + step).start()

    for step in range(pools):
        @pl.when((p - step >= 0) & (p < pools - 1))
        def _(step=step):
            shift(p - step, 0).wait_send()

        @pl.when((p + step < pools) & (p > 0))
        def _(step=step):
            shift(p + step, 1).wait_send()

    for origin in range(pools):
        store(origin).wait()


def solution(mesh):
    pools = mesh.shape["pool"]

    def body(hidden, k_cache, v_cache, lengths, expert_ids, w_query, w_key, w_value, w_out, w_router, w_gate, w_up, w_down):
        layers, shard, seq, kv_heads, head = k_cache.shape
        model = hidden.shape[1]
        toks = shard // pools
        local, ff = w_gate.shape[1], w_gate.shape[3]
        heads = w_query.shape[2] // head
        dims = (layers, toks, model, ff, heads, local)
        cos_t, sin_t = rotary_tables(seq + 8)
        f32, bf16 = jnp.float32, jnp.bfloat16
        d_chunks = model // CHUNK
        dma, vmem = pltpu.SemaphoreType.DMA, pltpu.VMEM
        scratch = [
            vmem((model, heads * head), bf16), vmem((model, 2 * kv_heads * head), bf16), vmem((heads * head, model), bf16),
            vmem((toks, seq * kv_heads, head), bf16), vmem((toks, seq * kv_heads, head), bf16),
            vmem((GU_SLOTS, 2, model, CHUNK), bf16), vmem((DOWN_SLOTS, ff, CHUNK), bf16),
            vmem((layers, 4 * toks, model), bf16), vmem((local, 4 * toks, ff), bf16),
            vmem((d_chunks, 4 * toks, CHUNK), f32),
            vmem((layers, d_chunks, toks, CHUNK), f32), vmem((layers, d_chunks, toks, CHUNK), f32),
            vmem((d_chunks, toks, CHUNK), f32), vmem((layers, d_chunks, toks, CHUNK), f32),
            vmem((pools, toks, model), bf16), vmem((toks, model), bf16),
            vmem((16 * toks, head), f32), vmem((16 * toks, head), f32), vmem((16 * toks, head), f32), vmem((16 * toks, head), f32),
            vmem((toks, heads * head), bf16), vmem((layers, 4 * toks, LANES), f32), vmem((local, 4 * toks, LANES), f32),
            vmem((layers, w_router.shape[2], model), f32),
            vmem(cos_t.shape, f32), vmem(sin_t.shape, f32), vmem((toks, head), f32), vmem((toks, head), f32),
            vmem((layers, 2, toks, LANES), jnp.int32),
            dma((4,)), dma((KV_BLOCKS, 2)), dma((GU_SLOTS, 2)), dma((DOWN_SLOTS,)), dma((4,)),
            dma((3,)), dma((layers, 3)), dma((3,)), dma((layers, 3)),
            dma((d_chunks,)), dma((layers, d_chunks)), dma((d_chunks,)), dma((layers, d_chunks)),
            dma((d_chunks,)), dma((layers, d_chunks)), dma((2, pools)), dma((pools,)), dma((pools,)),
        ]
        smem = pl.BlockSpec(memory_space=pltpu.SMEM)
        anyw = pl.BlockSpec(memory_space=pl.ANY)
        return pl.pallas_call(
            functools.partial(kernel, dims),
            out_shape=jax.ShapeDtypeStruct((shard, model), bf16),
            in_specs=[smem, smem] + [anyw] * 13,
            out_specs=anyw,
            scratch_shapes=scratch,
            compiler_params=pltpu.CompilerParams(collective_id=0, has_side_effects=True, vmem_limit_bytes=67043328),
            name="decode",
        )(lengths, jnp.swapaxes(expert_ids, 1, 2), hidden,
          k_cache.reshape(layers, shard, seq * kv_heads, head), v_cache.reshape(layers, shard, seq * kv_heads, head),
          w_query, w_key, w_value, w_out, jnp.swapaxes(w_router, 1, 2), jnp.asarray(cos_t), jnp.asarray(sin_t),
          w_gate, w_up, w_down)

    rows_spec = ("dp", "ep")
    in_specs = (P(rows_spec, None), P(None, rows_spec), P(None, rows_spec), P(rows_spec), P(None, rows_spec, None), P(), P(), P(), P(), P(), P(None, "ep"), P(None, "ep"), P(None, "ep"))
    return jax.shard_map(body, mesh=mesh, in_specs=in_specs, out_specs=P(rows_spec, None), check_vma=False)
```

time: 994 us -> 159 us (0.16)
  waiting for transfers between devices: 394 us -> 0 us
  starting transfers between devices: 281 us -> 0 us
  local copies, waits for them, and re-layouts: 222 us -> 2.06 us
  Pallas kernels: 0 us -> 157 us
  matrix products: 48.4 us -> 0 us
  other arithmetic: 24.8 us -> 0 us
  between operations: 14.5 us -> 0.01 us
    all_to_all x4 -> x0, waiting for transfers between devices: 339 us -> none  [the longest x2 174 us: body(): arrived = lax.all_to_all(dispatch_buf, ('pool', 'ep'), 0, 0, tiled=True)]
    all_to_all x4 -> x0, starting transfers between devices: 280 us -> none  [the longest x2 254 us: body(): came_back = lax.all_to_all(return_buf, ('pool', 'ep'), 0, 0, tiled=True)]
    pallas_call x0 -> x1, Pallas kernels: none -> 157 us  [body(): pl.pallas_call(functools.partial(kernel, dims), out_shape=jax.ShapeDtypeS...]
    another operation x13 -> x0, local copies, waits for them, and re-layouts: 121 us -> none
    slice x15 -> x0, local copies, waits for them, and re-layouts: 68.9 us -> none  [the longest x2 28.2 us: body(): vals_blk = lax.dynamic_slice_in_dim(v_cache[layer], start, tok_count, 0)]
    all_gather x1 -> x0, waiting for transfers between devices: 54.4 us -> none  [body(): gathered = lax.all_gather(state, 'pool', axis=0, tiled=True)]
    dot_general x18 -> x0, matrix products: 48.4 us -> none  [the longest x2 17.8 us: attend(): jnp.einsum('tkgd,tskd->tkgs', query, keys_blk, preferred_element_type=jnp...]
    concatenate x10 -> x0, local copies, waits for them, and re-layouts: 13.1 us -> none  [the longest x2 5.15 us: body(): return_buf = jnp.concatenate([produced, jnp.zeros_like(produced)], axis=0)]
  transfers between devices with their start and end apart: 5 -> 0, of which waited for: 5 -> 0; matrix products, arithmetic and copies ran while one was open for 1% -> 0% of each run, Pallas kernels for 0% -> 0%
where the time goes in v1:
time: 159 us
  Pallas kernels  157 us (99%)
  local copies, waits for them, and re-layouts  2.06 us (1%)
    pallas_call x1, Pallas kernels, body(): pl.pallas_call(functools.partial(kernel, dims), out_shape=jax.ShapeDtypeS...  157 us

profile of v1, /device:TPU:0, one launch (start us, length us, event | category | flops | bytes accessed | tf_op | source)
XLA Modules:
  0.0 158.8 jit_solution(7088490995905764090)
XLA Ops:
  0.0 156.8 %decode.1 = bf16[256,1536]{1,0:T(8,128)(2,1)} custom-call(s32[256]{0:T(256)} %lens.1, s32[2,2,256]{2,1,0:T(2,128)} %bitcast.7, bf16[256,1536]{1,0:T(8,128)(2,1)} %hid.1, bf16[2,256,256,128]{3,2,1,0:T(8,128)(2,1)} %bitcast.4, bf16[2,256,256,128]{3,2,1,0:T(8,128)(2,1)} %bitcast.5, bf16[2,1536,1536]{2,1,0:T(8,128)(2,1)} %wq.1, bf16[2,1536,256]{2,1,0:T(8,128)(2,1)} %wk.1, ...), custom_call_target="tpu_custom_call" | custom-call | tf_op jit(solution)/shard_map/decode/pallas_call | solution.py:431
  156.8 2.1 %copy.17 = bf16[256,1536]{1,0:T(8,128)(2,1)} copy(bf16[256,1536]{1,0:T(8,128)(2,1)} %decode.1) | data formatting | bytes 1572864

commit v2 on v1

v2 whole, which is shorter than its diff:
```python
import functools
import math

import jax
import jax.numpy as jnp
import numpy as np
from jax import lax
from jax.experimental import pallas as pl
from jax.experimental.pallas import tpu as pltpu
from jax.sharding import PartitionSpec as P

EPSILON = 1e-6
ROPE_BASE = 10000.0
MESH = pl.DeviceIdType.MESH
HEAD = 128
KV = 2
LANES = 128
CHUNK = 512
GU_SLOTS = 5
DOWN_SLOTS = 3
DOWN_COLS = 256
KV_BLOCKS = 4
GROUP = 8
LAG = 4


def rotary_tables(size):
    half = HEAD // 2
    freqs = np.float32(ROPE_BASE) ** (np.float32(-2.0) * np.arange(half, dtype=np.float32) / np.float32(HEAD))
    angle = np.arange(size, dtype=np.float32)[:, None] * freqs[None, :].astype(np.float32)
    cosine = np.cos(angle).astype(np.float32)
    sine = np.sin(angle).astype(np.float32)
    return np.concatenate([cosine, cosine], 1), np.concatenate([-sine, sine], 1)


def normed(values):
    return values * lax.rsqrt(jnp.mean(values * values, axis=-1, keepdims=True) + EPSILON)


def kernel(dims, lens, ids, hid, kc, vc, wq, wk, wv, wo, wr, cos_t, sin_t, wg, wu, wd, out,
           wq_b, wkv_b, wo_b, kbuf, vbuf, gu, dbuf, ubuf, inner, stage, part_l, part_m, merged, far, xg, acc_a,
           q2d, k2d, v2d, o2d, s_even, s_odd, att, gbuf, gsel, wr_b, cosb, sinb, cosr, sinr, id_b,
           wsem, kvsem, gusem, dsem, isem, us, ur, gs, gr, ps, pr, ms, mr, fs, fr, zs, zr, osem):
    layers, toks, model, ff, heads, local = dims
    e = lax.axis_index("ep")
    p = lax.axis_index("pool")
    pools = 4
    partner = e + 1 - 2 * (e % 2)
    cross = (e + 2) % 4
    start = p * toks
    ff_chunks = ff // CHUNK
    gu_total = local * ff_chunks
    d_chunks = model // DOWN_COLS
    rows = 4 * toks
    half = toks // 2
    group = heads // KV
    seq2 = kbuf.shape[1]
    per_block = toks // KV_BLOCKS

    def remote(src, dst, ssem, rsem, axis, index):
        return pltpu.make_async_remote_copy(src_ref=src, dst_ref=dst, send_sem=ssem, recv_sem=rsem,
                                            device_id={axis: index}, device_id_type=MESH)

    def columns(j):
        return pl.ds(pl.multiple_of(j * DOWN_COLS, DOWN_COLS), DOWN_COLS)

    def gu_copies(g):
        layer, i, slot = g // gu_total, g % gu_total, g % GU_SLOTS
        expert, c = i // ff_chunks, i % ff_chunks
        cols = pl.ds(pl.multiple_of(c * CHUNK, CHUNK), CHUNK)
        return [pltpu.make_async_copy(w.at[layer, expert, :, cols], gu.at[slot, k], gusem.at[slot, k])
                for k, w in enumerate((wg, wu))]

    def d_copies(d):
        layer, j, slot = d // d_chunks, d % d_chunks, d % DOWN_SLOTS
        return [pltpu.make_async_copy(wd.at[layer, k, :, columns(j)], dbuf.at[slot, k], dsem.at[slot, k]) for k in range(local)]

    kvw = KV * HEAD

    def weight_copies(layer):
        return [pltpu.make_async_copy(wq.at[layer], wq_b, wsem.at[0]),
                pltpu.make_async_copy(wk.at[layer], wkv_b.at[:, pl.ds(0, kvw)], wsem.at[1]),
                pltpu.make_async_copy(wv.at[layer], wkv_b.at[:, pl.ds(kvw, kvw)], wsem.at[2]),
                pltpu.make_async_copy(wo.at[layer], wo_b, wsem.at[3])]

    def kv_copies(layer, b):
        here = pl.ds(start + b * per_block, per_block)
        there = pl.ds(b * per_block, per_block)
        return [pltpu.make_async_copy(kc.at[layer, here], kbuf.at[there], kvsem.at[b, 0]),
                pltpu.make_async_copy(vc.at[layer, here], vbuf.at[there], kvsem.at[b, 1])]

    def start_attention(layer):
        copies = weight_copies(layer)
        for c in copies[:3]:
            c.start()
        for b in range(KV_BLOCKS):
            for c in kv_copies(layer, b):
                c.start()
        copies[3].start()

    first = [pltpu.make_async_copy(hid.at[pl.ds(start, toks)], acc_a, isem.at[0]),
             pltpu.make_async_copy(wr, wr_b, isem.at[1]),
             pltpu.make_async_copy(cos_t, cosb, isem.at[2]),
             pltpu.make_async_copy(sin_t, sinb, isem.at[3])]
    for c in first:
        c.start()
    start_attention(0)

    barrier = pltpu.get_barrier_semaphore()
    pl.semaphore_signal(barrier, inc=1, device_id={"ep": partner}, device_id_type=MESH)
    pl.semaphore_signal(barrier, inc=1, device_id={"ep": cross}, device_id_type=MESH)

    @pl.when(p > 0)
    def _():
        pl.semaphore_signal(barrier, inc=1, device_id={"pool": p - 1}, device_id_type=MESH)

    @pl.when(p < pools - 1)
    def _():
        pl.semaphore_signal(barrier, inc=1, device_id={"pool": p + 1}, device_id_type=MESH)

    middle = (p > 0) & (p < pools - 1)

    @pl.when(middle)
    def _():
        pl.semaphore_wait(barrier, 4)

    @pl.when(jnp.logical_not(middle))
    def _():
        pl.semaphore_wait(barrier, 3)

    for c in first:
        c.wait()

    zeros = jnp.zeros(((16 - heads) * toks, HEAD), jnp.float32)
    for ref in (q2d, k2d, v2d):
        ref[pl.ds(heads * toks, (16 - heads) * toks), :] = zeros

    def spread(t, carry):
        where = pl.ds(t, 1)
        n = lens[start + t]
        cosr[where, :] = cosb[pl.ds(n, 1), :]
        sinr[where, :] = sinb[pl.ds(n, 1), :]
        for layer in range(layers):
            for k in range(2):
                id_b[layer, k, where, :] = jnp.full((1, LANES), ids[layer, k, start + t], jnp.int32)
        return carry

    lax.fori_loop(0, toks, spread, 0)

    lane = lax.broadcasted_iota(jnp.int32, (16, seq2), 1)
    head_kv = jnp.where(lax.broadcasted_iota(jnp.int32, (16, seq2), 0) >= group, 1, 0)
    parity = (lane % KV) == head_kv
    scale = HEAD ** -0.5

    def layer_body(layer, carry):
        hidden = acc_a[...].astype(jnp.float32)
        h = normed(hidden).astype(jnp.bfloat16)
        copies = weight_copies(layer)
        copies[0].wait()
        cosine, sine = cosr[...], sinr[...]

        def rope(v):
            return (v * cosine + pltpu.roll(v, HEAD // 2, 1) * sine).astype(jnp.bfloat16).astype(jnp.float32)

        for n in range(heads * HEAD // CHUNK):
            qn = jnp.dot(h, wq_b[:, n * CHUNK:(n + 1) * CHUNK], preferred_element_type=jnp.float32)
            for k in range(CHUNK // HEAD):
                head = n * (CHUNK // HEAD) + k
                q2d[pl.ds(head * toks, toks), :] = rope(qn[:, k * HEAD:(k + 1) * HEAD])
        copies[1].wait()
        copies[2].wait()
        kv = jnp.dot(h, wkv_b[...], preferred_element_type=jnp.float32)
        for j in range(KV):
            kj = rope(kv[:, j * HEAD:(j + 1) * HEAD])
            vj = kv[:, kvw + j * HEAD:kvw + (j + 1) * HEAD].astype(jnp.bfloat16).astype(jnp.float32)
            for k in range(group):
                at = pl.ds((j * group + k) * toks, toks)
                k2d[at, :] = kj
                v2d[at, :] = vj

        @pl.when(layer == 0)
        def _():
            for g in range(GU_SLOTS):
                for c in gu_copies(g):
                    c.start()

        def score(first_token, ref):
            for k in range(GROUP):
                q = q2d[pl.ds(first_token + k, 16, stride=toks), :].astype(jnp.bfloat16)
                ref[k * 16:(k + 1) * 16, :] = lax.dot_general(q, kbuf[first_token + k], (((1,), (1,)), ((), ())),
                                                              preferred_element_type=jnp.float32)

        def mix(first_token, ref):
            weights, news, totals = [], [], []
            for k in range(GROUP):
                at = pl.ds(first_token + k, 16, stride=toks)
                n2 = lens[start + first_token + k] * KV
                s = jnp.where(parity & (lane < n2), ref[k * 16:(k + 1) * 16, :] * scale, -jnp.inf)
                s_new = jnp.sum(q2d[at, :] * k2d[at, :], axis=1, keepdims=True) * scale
                peak = jnp.maximum(jnp.max(s, axis=1, keepdims=True), s_new)
                w = jnp.exp(s - peak)
                w_new = jnp.exp(s_new - peak)
                totals.append(jnp.sum(w, axis=1, keepdims=True) + w_new)
                weights.append(w.astype(jnp.bfloat16))
                news.append(w_new.astype(jnp.bfloat16).astype(jnp.float32))
            sums = [jnp.dot(weights[k], vbuf[first_token + k], preferred_element_type=jnp.float32) for k in range(GROUP)]
            for k in range(GROUP):
                at = pl.ds(first_token + k, 16, stride=toks)
                o2d[at, :] = (sums[k] + news[k] * v2d[at, :]) / totals[k]

        kv_copies(layer, 0)[0].wait()
        score(0, s_even)

        def attend(i, carry):
            kv_copies(layer, i)[1].wait()

            @pl.when(i + 1 < KV_BLOCKS)
            def _():
                kv_copies(layer, i + 1)[0].wait()

            t = i * per_block
            score(t + GROUP, s_odd)
            mix(t, s_even)
            score((t + 2 * GROUP) % toks, s_even)
            mix(t + GROUP, s_odd)
            return carry

        lax.fori_loop(0, KV_BLOCKS, attend, 0)

        @pl.when(layer == 0)
        def _():
            for d in range(DOWN_SLOTS):
                for c in d_copies(d):
                    c.start()

        for head in range(heads):
            att[:, head * HEAD:(head + 1) * HEAD] = o2d[pl.ds(head * toks, toks), :].astype(jnp.bfloat16)
        copies[3].wait()
        for n in range(model // CHUNK):
            cols = slice(n * CHUNK, (n + 1) * CHUNK)
            a = acc_a[:, cols].astype(jnp.float32) + jnp.dot(att[...], wo_b[:, cols], preferred_element_type=jnp.float32)
            acc_a[:, cols] = a.astype(jnp.bfloat16)

        u = normed(acc_a[...].astype(jnp.float32)).astype(jnp.bfloat16)
        ubuf[layer, pl.ds(0, toks), :] = u

        def block(ref, b):
            return ref.at[layer, pl.ds(b * toks, toks)]

        def piece(b, h):
            return ubuf.at[layer, pl.ds(b * toks + h * half, half)]

        u_near = [remote(piece(0, h), piece(1, h), us.at[0, h], ur.at[layer, 0, h], "ep", partner) for h in range(2)]
        u_far = [remote(piece(0, h), piece(2, h), us.at[1, h], ur.at[layer, 1, h], "ep", cross) for h in range(2)]
        u_pass = [remote(piece(2, h), piece(3, h), us.at[2, h], ur.at[layer, 2, h], "ep", partner) for h in range(2)]
        g_near = remote(block(gbuf, 0), block(gbuf, 1), gs.at[0], gr.at[layer, 0], "ep", partner)
        g_far = remote(block(gbuf, 0), block(gbuf, 2), gs.at[1], gr.at[layer, 1], "ep", cross)
        g_pass = remote(block(gbuf, 2), block(gbuf, 3), gs.at[2], gr.at[layer, 2], "ep", partner)
        for c in u_far + u_near:
            c.start()

        wl = wr_b[layer]
        hi = wl.astype(jnp.bfloat16).astype(jnp.float32)
        rest = wl - hi
        mid = rest.astype(jnp.bfloat16).astype(jnp.float32)
        low = rest - mid
        wide = jnp.concatenate([hi, mid, low, jnp.zeros((LANES - 3 * wl.shape[0], model), jnp.float32)], axis=0).astype(jnp.bfloat16)
        parts = lax.dot_general(u, wide, (((1,), (1,)), ((), ())), preferred_element_type=jnp.float32)
        logits = parts + pltpu.roll(parts, LANES - 8, 1) + pltpu.roll(parts, LANES - 16, 1)
        expert_lane = lax.broadcasted_iota(jnp.int32, (toks, LANES), 1)
        chosen = (id_b[layer, 0] == expert_lane) | (id_b[layer, 1] == expert_lane)
        logits = jnp.where(chosen, logits, -jnp.inf)
        ew = jnp.exp(logits - jnp.max(logits, axis=1, keepdims=True))
        gbuf[layer, pl.ds(0, toks), :] = ew / jnp.sum(ew, axis=1, keepdims=True)
        g_far.start()
        g_near.start()

        def gate_up(low, count, wait, release):
            def step(i, carry):
                g = layer * gu_total + i
                slot = g % GU_SLOTS
                if wait:
                    for c in gu_copies(g):
                        c.wait()
                tokens = ubuf[layer, low:low + count, :]
                one = jnp.dot(tokens, gu[slot, 0], preferred_element_type=jnp.float32)
                three = jnp.dot(tokens, gu[slot, 1], preferred_element_type=jnp.float32)
                cols = pl.ds(pl.multiple_of((i % ff_chunks) * CHUNK, CHUNK), CHUNK)
                inner[i // ff_chunks, low:low + count, cols] = (jax.nn.silu(one) * three).astype(jnp.bfloat16)
                if release:
                    @pl.when(g + GU_SLOTS < layers * gu_total)
                    def _():
                        for c in gu_copies(g + GU_SLOTS):
                            c.start()

                return carry

            return step

        for c in u_near:
            c.wait_recv()
        lax.fori_loop(0, 3, gate_up(0, 2 * toks, True, False), 0)
        u_far[0].wait_recv()
        u_pass[0].start()
        lax.fori_loop(3, GU_SLOTS, gate_up(0, 2 * toks, True, False), 0)
        u_far[1].wait_recv()
        u_pass[1].start()
        g_far.wait_recv()
        g_pass.start()
        for c in u_pass:
            c.wait_recv()
        lax.fori_loop(0, GU_SLOTS, gate_up(2 * toks, 2 * toks, False, True), 0)
        lax.fori_loop(GU_SLOTS, gu_total, gate_up(0, 4 * toks, True, True), 0)

        g_near.wait_recv()
        g_pass.wait_recv()
        gates = gbuf[layer]
        row_lane = lax.broadcasted_iota(jnp.int32, (rows, LANES), 1)
        for k in range(local):
            one = jnp.sum(jnp.where(row_lane == e * local + k, gates, 0.0), axis=1, keepdims=True)
            gsel[k] = jnp.broadcast_to(one, (rows, LANES))

        @pl.when(layer + 1 < layers)
        def _():
            start_attention(layer + 1)

        def near_l(j):
            return remote(stage.at[j, pl.ds(toks, toks)], part_l.at[layer, j], ps.at[j], pr.at[layer, j], "ep", partner)

        def near_m(j):
            return remote(stage.at[j, pl.ds(3 * toks, toks)], part_m.at[layer, j], ms.at[j], mr.at[layer, j], "ep", partner)

        def far_copy(j):
            return remote(merged.at[j], far.at[layer, j], fs.at[j], fr.at[layer, j], "ep", cross)

        def merge(j):
            near_m(j).wait_recv()
            merged[j] = stage[j, pl.ds(2 * toks, toks), :] + part_m[layer, j]
            far_copy(j).start()

        def combine(c):
            near_l(c).wait_recv()
            far_copy(c).wait_recv()
            total = (stage[c, pl.ds(0, toks), :] + part_l[layer, c]) + far[layer, c]
            x = (acc_a[:, columns(c)].astype(jnp.float32) + total).astype(jnp.bfloat16)
            acc_a[:, columns(c)] = x

            @pl.when(layer == layers - 1)
            def _():
                xg[p, :, columns(c)] = x
                store(p, c).start()

                @pl.when(p < pools - 1)
                def _():
                    shift(p, c, 0).start()

                @pl.when(p > 0)
                def _():
                    shift(p, c, 1).start()

        def down(j, slot, low):
            terms = [None] * (DOWN_COLS // LANES)
            for k in range(local):
                y = jnp.dot(inner[k, low:low + 2 * toks, :], dbuf[slot, k], preferred_element_type=jnp.float32)
                y = y.astype(jnp.bfloat16).astype(jnp.float32)
                gate = gsel[k, low:low + 2 * toks, :]
                for n in range(len(terms)):
                    term = jnp.where(gate > 0.0, gate * y[:, n * LANES:(n + 1) * LANES], 0.0)
                    terms[n] = term if k == 0 else terms[n] + term
            for n in range(len(terms)):
                stage[j, low:low + 2 * toks, n * LANES:(n + 1) * LANES] = terms[n]

        def down_body(j, carry):
            d = layer * d_chunks + j
            slot = d % DOWN_SLOTS
            for c in d_copies(d):
                c.wait()
            down(j, slot, 2 * toks)
            near_m(j).start()

            @pl.when(j > 0)
            def _():
                merge(j - 1)

            down(j, slot, 0)
            near_l(j).start()

            @pl.when(d + DOWN_SLOTS < layers * d_chunks)
            def _():
                for c in d_copies(d + DOWN_SLOTS):
                    c.start()

            @pl.when(j >= LAG)
            def _():
                combine(j - LAG)

            return carry

        lax.fori_loop(0, d_chunks, down_body, 0)
        merge(d_chunks - 1)

        def last_ones(c, carry):
            combine(c)
            return carry

        lax.fori_loop(d_chunks - LAG, d_chunks, last_ones, 0)

        for c in u_near + u_far + u_pass + [g_near, g_far, g_pass]:
            c.wait_send()

        def sent(j, carry):
            near_l(j).wait_send()
            near_m(j).wait_send()
            far_copy(j).wait_send()
            return carry

        lax.fori_loop(0, d_chunks, sent, 0)
        return carry

    def shift(origin, c, way):
        at = xg.at[origin, :, columns(c)]
        return remote(at, at, zs.at[way, origin, c], zr.at[origin, c], "pool", p + 1 - 2 * way)

    def store(origin, c):
        here = pl.ds(origin * toks, toks)
        return pltpu.make_async_copy(xg.at[origin, :, columns(c)], out.at[here, columns(c)], osem.at[origin, c])

    lax.fori_loop(0, layers, layer_body, 0)

    def wave(i, carry):
        for step in range(1, pools):
            c = i - (step - 1)
            live = (c >= 0) & (c < d_chunks)

            @pl.when(live & (p - step >= 0))
            def _(step=step, c=c):
                shift(p - step, c, 0).wait_recv()

                @pl.when(p < pools - 1)
                def _():
                    shift(p - step, c, 0).start()

                store(p - step, c).start()

            @pl.when(live & (p + step < pools))
            def _(step=step, c=c):
                shift(p + step, c, 1).wait_recv()

                @pl.when(p > 0)
                def _():
                    shift(p + step, c, 1).start()

                store(p + step, c).start()

        return carry

    lax.fori_loop(0, d_chunks + pools - 2, wave, 0)

    def finish(c, carry):
        for step in range(pools):
            @pl.when((p - step >= 0) & (p < pools - 1))
            def _(step=step):
                shift(p - step, c, 0).wait_send()

            @pl.when((p + step < pools) & (p > 0))
            def _(step=step):
                shift(p + step, c, 1).wait_send()

        for origin in range(pools):
            store(origin, c).wait()
        return carry

    lax.fori_loop(0, d_chunks, finish, 0)


def solution(mesh):
    pools = mesh.shape["pool"]

    def body(hidden, k_cache, v_cache, lengths, expert_ids, w_query, w_key, w_value, w_out, w_router, w_gate, w_up, w_down):
        layers, shard, seq, kv_heads, head = k_cache.shape
        model = hidden.shape[1]
        toks = shard // pools
        local, ff = w_gate.shape[1], w_gate.shape[3]
        heads = w_query.shape[2] // head
        dims = (layers, toks, model, ff, heads, local)
        cos_t, sin_t = rotary_tables(seq + 8)
        f32, bf16 = jnp.float32, jnp.bfloat16
        d_chunks = model // DOWN_COLS
        dma, vmem = pltpu.SemaphoreType.DMA, pltpu.VMEM
        scratch = [
            vmem((model, heads * head), bf16), vmem((model, 2 * kv_heads * head), bf16), vmem((heads * head, model), bf16),
            vmem((toks, seq * kv_heads, head), bf16), vmem((toks, seq * kv_heads, head), bf16),
            vmem((GU_SLOTS, 2, model, CHUNK), bf16), vmem((DOWN_SLOTS, local, ff, DOWN_COLS), bf16),
            vmem((layers, 4 * toks, model), bf16), vmem((local, 4 * toks, ff), bf16),
            vmem((d_chunks, 4 * toks, DOWN_COLS), f32),
            vmem((layers, d_chunks, toks, DOWN_COLS), f32), vmem((layers, d_chunks, toks, DOWN_COLS), f32),
            vmem((d_chunks, toks, DOWN_COLS), f32), vmem((layers, d_chunks, toks, DOWN_COLS), f32),
            vmem((pools, toks, model), bf16), vmem((toks, model), bf16),
            vmem((16 * toks, head), f32), vmem((16 * toks, head), f32), vmem((16 * toks, head), f32), vmem((16 * toks, head), f32),
            vmem((GROUP * 16, seq * kv_heads), f32), vmem((GROUP * 16, seq * kv_heads), f32),
            vmem((toks, heads * head), bf16), vmem((layers, 4 * toks, LANES), f32), vmem((local, 4 * toks, LANES), f32),
            vmem((layers, w_router.shape[2], model), f32),
            vmem(cos_t.shape, f32), vmem(sin_t.shape, f32), vmem((toks, head), f32), vmem((toks, head), f32),
            vmem((layers, 2, toks, LANES), jnp.int32),
            dma((4,)), dma((KV_BLOCKS, 2)), dma((GU_SLOTS, 2)), dma((DOWN_SLOTS, local)), dma((4,)),
            dma((3, 2)), dma((layers, 3, 2)), dma((3,)), dma((layers, 3)),
            dma((d_chunks,)), dma((layers, d_chunks)), dma((d_chunks,)), dma((layers, d_chunks)),
            dma((d_chunks,)), dma((layers, d_chunks)), dma((2, pools, d_chunks)), dma((pools, d_chunks)), dma((pools, d_chunks)),
        ]
        smem = pl.BlockSpec(memory_space=pltpu.SMEM)
        anyw = pl.BlockSpec(memory_space=pl.ANY)
        return pl.pallas_call(
            functools.partial(kernel, dims),
            out_shape=jax.ShapeDtypeStruct((shard, model), bf16),
            in_specs=[smem, smem] + [anyw] * 13,
            out_specs=anyw,
            scratch_shapes=scratch,
            compiler_params=pltpu.CompilerParams(collective_id=0, has_side_effects=True, vmem_limit_bytes=67043328),
            name="decode",
        )(lengths, jnp.swapaxes(expert_ids, 1, 2), hidden,
          k_cache.reshape(layers, shard, seq * kv_heads, head), v_cache.reshape(layers, shard, seq * kv_heads, head),
          w_query, w_key, w_value, w_out, jnp.swapaxes(w_router, 1, 2), jnp.asarray(cos_t), jnp.asarray(sin_t),
          w_gate, w_up, w_down)

    rows_spec = ("dp", "ep")
    in_specs = (P(rows_spec, None), P(None, rows_spec), P(None, rows_spec), P(rows_spec), P(None, rows_spec, None), P(), P(), P(), P(), P(), P(None, "ep"), P(None, "ep"), P(None, "ep"))
    return jax.shard_map(body, mesh=mesh, in_specs=in_specs, out_specs=P(rows_spec, None), check_vma=False)
```

time: 159 us -> 113 us (0.71)
  Pallas kernels: 157 us -> 111 us
    pallas_call x1, Pallas kernels: 157 us -> 111 us  [body(): pl.pallas_call(functools.partial(kernel, dims), out_shape=jax.ShapeDtypeS...]
where the time goes in v2:
time: 113 us
  Pallas kernels  111 us (98%)
  local copies, waits for them, and re-layouts  2.06 us (2%)
    pallas_call x1, Pallas kernels, body(): pl.pallas_call(functools.partial(kernel, dims), out_shape=jax.ShapeDtypeS...  111 us

profile of v2, /device:TPU:0, one launch (start us, length us, event | category | flops | bytes accessed | tf_op | source)
XLA Modules:
  0.0 112.6 jit_solution(9387222321287024661)
XLA Ops:
  0.0 110.6 %decode.1 = bf16[256,1536]{1,0:T(8,128)(2,1)} custom-call(s32[256]{0:T(256)} %lens.1, s32[2,2,256]{2,1,0:T(2,128)} %bitcast.7, bf16[256,1536]{1,0:T(8,128)(2,1)} %hid.1, bf16[2,256,256,128]{3,2,1,0:T(8,128)(2,1)} %bitcast.4, bf16[2,256,256,128]{3,2,1,0:T(8,128)(2,1)} %bitcast.5, bf16[2,1536,1536]{2,1,0:T(8,128)(2,1)} %wq.1, bf16[2,1536,256]{2,1,0:T(8,128)(2,1)} %wk.1, ...), custom_call_target="tpu_custom_call" | custom-call | tf_op jit(solution)/shard_map/decode/pallas_call | solution.py:512
  110.6 2.1 %copy.17 = bf16[256,1536]{1,0:T(8,128)(2,1)} copy(bf16[256,1536]{1,0:T(8,128)(2,1)} %decode.1) | data formatting | bytes 1572864

commit v3 on v2

--- a/solution.py
+++ b/solution.py
@@ -16,12 +16,17 @@
 KV = 2
 LANES = 128
 CHUNK = 512
-GU_SLOTS = 5
+GU_COLS = 1024
+GU_SLOTS = 4
+PIECE = 256
 DOWN_SLOTS = 3
 DOWN_COLS = 256
 KV_BLOCKS = 4
 GROUP = 8
 LAG = 4
+ATTENTION_AT = 3
+WAYS = (-2, 2, -1, 1)
+RELAY_LAG = 2
 
 
 def rotary_tables(size):
@@ -38,7 +43,7 @@
 
 
 def kernel(dims, lens, ids, hid, kc, vc, wq, wk, wv, wo, wr, cos_t, sin_t, wg, wu, wd, out,
-           wq_b, wkv_b, wo_b, kbuf, vbuf, gu, dbuf, ubuf, inner, stage, part_l, part_m, merged, far, xg, acc_a,
+           wo_b, kbuf, vbuf, gu, dbuf, ubuf, inner, stage, part_l, part_m, merged, far, xg, acc_a,
            q2d, k2d, v2d, o2d, s_even, s_odd, att, gbuf, gsel, wr_b, cosb, sinb, cosr, sinr, id_b,
            wsem, kvsem, gusem, dsem, isem, us, ur, gs, gr, ps, pr, ms, mr, fs, fr, zs, zr, osem):
     layers, toks, model, ff, heads, local = dims
@@ -48,7 +53,7 @@
     partner = e + 1 - 2 * (e % 2)
     cross = (e + 2) % 4
     start = p * toks
-    ff_chunks = ff // CHUNK
+    ff_chunks = ff // GU_COLS
     gu_total = local * ff_chunks
     d_chunks = model // DOWN_COLS
     rows = 4 * toks
@@ -65,23 +70,28 @@
         return pl.ds(pl.multiple_of(j * DOWN_COLS, DOWN_COLS), DOWN_COLS)
 
     def gu_copies(g):
-        layer, i, slot = g // gu_total, g % gu_total, g % GU_SLOTS
+        layer, i, slot = g // gu_total, g % gu_total, (g % gu_total) % GU_SLOTS
         expert, c = i // ff_chunks, i % ff_chunks
-        cols = pl.ds(pl.multiple_of(c * CHUNK, CHUNK), CHUNK)
+        cols = pl.ds(pl.multiple_of(c * GU_COLS, GU_COLS), GU_COLS)
         return [pltpu.make_async_copy(w.at[layer, expert, :, cols], gu.at[slot, k], gusem.at[slot, k])
                 for k, w in enumerate((wg, wu))]
 
     def d_copies(d):
-        layer, j, slot = d // d_chunks, d % d_chunks, d % DOWN_SLOTS
+        layer, j, slot = d // d_chunks, d % d_chunks, (d % d_chunks) % DOWN_SLOTS
         return [pltpu.make_async_copy(wd.at[layer, k, :, columns(j)], dbuf.at[slot, k], dsem.at[slot, k]) for k in range(local)]
 
     kvw = KV * HEAD
+    q_cols = heads * HEAD
+
+    def proj(column, count):
+        return gu.at[GU_SLOTS - 1, column // GU_COLS, :, pl.ds(column % GU_COLS, count)]
 
     def weight_copies(layer):
-        return [pltpu.make_async_copy(wq.at[layer], wq_b, wsem.at[0]),
-                pltpu.make_async_copy(wk.at[layer], wkv_b.at[:, pl.ds(0, kvw)], wsem.at[1]),
-                pltpu.make_async_copy(wv.at[layer], wkv_b.at[:, pl.ds(kvw, kvw)], wsem.at[2]),
-                pltpu.make_async_copy(wo.at[layer], wo_b, wsem.at[3])]
+        pieces = range(q_cols // CHUNK)
+        return [pltpu.make_async_copy(wk.at[layer], proj(q_cols, kvw), wsem.at[0]),
+                pltpu.make_async_copy(wv.at[layer], proj(q_cols + kvw, kvw), wsem.at[1]),
+                pltpu.make_async_copy(wo.at[layer], wo_b, wsem.at[2]),
+                *(pltpu.make_async_copy(wq.at[layer, :, pl.ds(n * CHUNK, CHUNK)], proj(n * CHUNK, CHUNK), wsem.at[3 + n]) for n in pieces)]
 
     def kv_copies(layer, b):
         here = pl.ds(start + b * per_block, per_block)
@@ -89,44 +99,49 @@
         return [pltpu.make_async_copy(kc.at[layer, here], kbuf.at[there], kvsem.at[b, 0]),
                 pltpu.make_async_copy(vc.at[layer, here], vbuf.at[there], kvsem.at[b, 1])]
 
-    def start_attention(layer):
+    def start_projections(layer):
         copies = weight_copies(layer)
-        for c in copies[:3]:
+        for c in copies[3:] + copies[:2]:
             c.start()
+
+    def start_caches(layer):
         for b in range(KV_BLOCKS):
             for c in kv_copies(layer, b):
                 c.start()
-        copies[3].start()
+        weight_copies(layer)[2].start()
+
+    def start_attention(layer):
+        start_projections(layer)
+        start_caches(layer)
+
+    def start_gate_up(layer):
+        for i in range(GU_SLOTS - 1):
+            for c in gu_copies(layer * gu_total + i):
+                c.start()
+
+    def start_down(layer):
+        for j in range(DOWN_SLOTS):
+            for c in d_copies(layer * d_chunks + j):
+                c.start()
 
     first = [pltpu.make_async_copy(hid.at[pl.ds(start, toks)], acc_a, isem.at[0]),
              pltpu.make_async_copy(wr, wr_b, isem.at[1]),
              pltpu.make_async_copy(cos_t, cosb, isem.at[2]),
              pltpu.make_async_copy(sin_t, sinb, isem.at[3])]
-    for c in first:
+    first[0].start()
+    start_projections(0)
+    for c in first[1:]:
         c.start()
-    start_attention(0)
 
     barrier = pltpu.get_barrier_semaphore()
     pl.semaphore_signal(barrier, inc=1, device_id={"ep": partner}, device_id_type=MESH)
     pl.semaphore_signal(barrier, inc=1, device_id={"ep": cross}, device_id_type=MESH)
 
-    @pl.when(p > 0)
-    def _():
-        pl.semaphore_signal(barrier, inc=1, device_id={"pool": p - 1}, device_id_type=MESH)
-
-    @pl.when(p < pools - 1)
-    def _():
-        pl.semaphore_signal(barrier, inc=1, device_id={"pool": p + 1}, device_id_type=MESH)
-
-    middle = (p > 0) & (p < pools - 1)
-
-    @pl.when(middle)
-    def _():
-        pl.semaphore_wait(barrier, 4)
-
-    @pl.when(jnp.logical_not(middle))
-    def _():
-        pl.semaphore_wait(barrier, 3)
+    inside = (p > 0) & (p < pools - 1)
+    for way in (-2, -1, 1, 2):
+        @pl.when((p + way >= 0) & (p + way < pools))
+        def _(way=way):
+            pl.semaphore_signal(barrier, inc=1, device_id={"pool": p + way}, device_id_type=MESH)
 
     for c in first:
         c.wait()
@@ -146,6 +161,7 @@
         return carry
 
     lax.fori_loop(0, toks, spread, 0)
+    start_caches(0)
 
     lane = lax.broadcasted_iota(jnp.int32, (16, seq2), 1)
     head_kv = jnp.where(lax.broadcasted_iota(jnp.int32, (16, seq2), 0) >= group, 1, 0)
@@ -156,20 +172,20 @@
         hidden = acc_a[...].astype(jnp.float32)
         h = normed(hidden).astype(jnp.bfloat16)
         copies = weight_copies(layer)
-        copies[0].wait()
         cosine, sine = cosr[...], sinr[...]
 
         def rope(v):
             return (v * cosine + pltpu.roll(v, HEAD // 2, 1) * sine).astype(jnp.bfloat16).astype(jnp.float32)
 
         for n in range(heads * HEAD // CHUNK):
-            qn = jnp.dot(h, wq_b[:, n * CHUNK:(n + 1) * CHUNK], preferred_element_type=jnp.float32)
+            copies[3 + n].wait()
+            qn = jnp.dot(h, proj(n * CHUNK, CHUNK)[...], preferred_element_type=jnp.float32)
             for k in range(CHUNK // HEAD):
                 head = n * (CHUNK // HEAD) + k
                 q2d[pl.ds(head * toks, toks), :] = rope(qn[:, k * HEAD:(k + 1) * HEAD])
+        copies[0].wait()
         copies[1].wait()
-        copies[2].wait()
-        kv = jnp.dot(h, wkv_b[...], preferred_element_type=jnp.float32)
+        kv = jnp.dot(h, proj(q_cols, 2 * kvw)[...], preferred_element_type=jnp.float32)
         for j in range(KV):
             kj = rope(kv[:, j * HEAD:(j + 1) * HEAD])
             vj = kv[:, kvw + j * HEAD:kvw + (j + 1) * HEAD].astype(jnp.bfloat16).astype(jnp.float32)
@@ -180,9 +196,10 @@
 
         @pl.when(layer == 0)
         def _():
-            for g in range(GU_SLOTS):
-                for c in gu_copies(g):
-                    c.start()
+            start_gate_up(0)
+
+        for c in gu_copies(layer * gu_total + GU_SLOTS - 1):
+            c.start()
 
         def score(first_token, ref):
             for k in range(GROUP):
@@ -229,13 +246,11 @@
 
         @pl.when(layer == 0)
         def _():
-            for d in range(DOWN_SLOTS):
-                for c in d_copies(d):
-                    c.start()
+            start_down(0)
 
         for head in range(heads):
             att[:, head * HEAD:(head + 1) * HEAD] = o2d[pl.ds(head * toks, toks), :].astype(jnp.bfloat16)
-        copies[3].wait()
+        copies[2].wait()
         for n in range(model // CHUNK):
             cols = slice(n * CHUNK, (n + 1) * CHUNK)
             a = acc_a[:, cols].astype(jnp.float32) + jnp.dot(att[...], wo_b[:, cols], preferred_element_type=jnp.float32)
@@ -256,6 +271,14 @@
         g_near = remote(block(gbuf, 0), block(gbuf, 1), gs.at[0], gr.at[layer, 0], "ep", partner)
         g_far = remote(block(gbuf, 0), block(gbuf, 2), gs.at[1], gr.at[layer, 1], "ep", cross)
         g_pass = remote(block(gbuf, 2), block(gbuf, 3), gs.at[2], gr.at[layer, 2], "ep", partner)
+        @pl.when((layer == 0) & inside)
+        def _():
+            pl.semaphore_wait(barrier, 5)
+
+        @pl.when((layer == 0) & jnp.logical_not(inside))
+        def _():
+            pl.semaphore_wait(barrier, 4)
+
         for c in u_far + u_near:
             c.start()
 
@@ -278,17 +301,18 @@
         def gate_up(low, count, wait, release):
             def step(i, carry):
                 g = layer * gu_total + i
-                slot = g % GU_SLOTS
+                slot = i % GU_SLOTS
                 if wait:
                     for c in gu_copies(g):
                         c.wait()
-                tokens = ubuf[layer, low:low + count, :]
-                one = jnp.dot(tokens, gu[slot, 0], preferred_element_type=jnp.float32)
-                three = jnp.dot(tokens, gu[slot, 1], preferred_element_type=jnp.float32)
-                cols = pl.ds(pl.multiple_of((i % ff_chunks) * CHUNK, CHUNK), CHUNK)
-                inner[i // ff_chunks, low:low + count, cols] = (jax.nn.silu(one) * three).astype(jnp.bfloat16)
+                for n in range(0, GU_COLS, PIECE):
+                    tokens = ubuf[layer, low:low + count, :]
+                    one = jnp.dot(tokens, gu[slot, 0, :, n:n + PIECE], preferred_element_type=jnp.float32)
+                    three = jnp.dot(tokens, gu[slot, 1, :, n:n + PIECE], preferred_element_type=jnp.float32)
+                    cols = pl.ds(pl.multiple_of((i % ff_chunks) * GU_COLS + n, PIECE), PIECE)
+                    inner[i // ff_chunks, low:low + count, cols] = (jax.nn.silu(one) * three).astype(jnp.bfloat16)
                 if release:
-                    @pl.when(g + GU_SLOTS < layers * gu_total)
+                    @pl.when(i + GU_SLOTS < gu_total)
                     def _():
                         for c in gu_copies(g + GU_SLOTS):
                             c.start()
@@ -299,10 +323,10 @@
 
         for c in u_near:
             c.wait_recv()
-        lax.fori_loop(0, 3, gate_up(0, 2 * toks, True, False), 0)
+        lax.fori_loop(0, 2, gate_up(0, 2 * toks, True, False), 0)
         u_far[0].wait_recv()
         u_pass[0].start()
-        lax.fori_loop(3, GU_SLOTS, gate_up(0, 2 * toks, True, False), 0)
+        lax.fori_loop(2, GU_SLOTS, gate_up(0, 2 * toks, True, False), 0)
         u_far[1].wait_recv()
         u_pass[1].start()
         g_far.wait_recv()
@@ -320,10 +344,6 @@
             one = jnp.sum(jnp.where(row_lane == e * local + k, gates, 0.0), axis=1, keepdims=True)
             gsel[k] = jnp.broadcast_to(one, (rows, LANES))
 
-        @pl.when(layer + 1 < layers)
-        def _():
-            start_attention(layer + 1)
-
         def near_l(j):
             return remote(stage.at[j, pl.ds(toks, toks)], part_l.at[layer, j], ps.at[j], pr.at[layer, j], "ep", partner)
 
@@ -350,13 +370,10 @@
                 xg[p, :, columns(c)] = x
                 store(p, c).start()
 
-                @pl.when(p < pools - 1)
-                def _():
-                    shift(p, c, 0).start()
-
-                @pl.when(p > 0)
-                def _():
-                    shift(p, c, 1).start()
+                for way in WAYS:
+                    @pl.when((p + way >= 0) & (p + way < pools))
+                    def _(way=way):
+                        spread_out(p, c, way).start()
 
         def down(j, slot, low):
             terms = [None] * (DOWN_COLS // LANES)
@@ -370,37 +387,54 @@
             for n in range(len(terms)):
                 stage[j, low:low + 2 * toks, n * LANES:(n + 1) * LANES] = terms[n]
 
+        def down_far(j):
+            for c in d_copies(layer * d_chunks + j):
+                c.wait()
+            down(j, j % DOWN_SLOTS, 2 * toks)
+            near_m(j).start()
+
         def down_body(j, carry):
             d = layer * d_chunks + j
-            slot = d % DOWN_SLOTS
-            for c in d_copies(d):
-                c.wait()
-            down(j, slot, 2 * toks)
-            near_m(j).start()
-
-            @pl.when(j > 0)
-            def _():
-                merge(j - 1)
-
-            down(j, slot, 0)
+
+            @pl.when(j + 1 < d_chunks)
+            def _():
+                down_far(j + 1)
+
+            merge(j)
+            down(j, j % DOWN_SLOTS, 0)
             near_l(j).start()
 
-            @pl.when(d + DOWN_SLOTS < layers * d_chunks)
+            @pl.when(j + DOWN_SLOTS < d_chunks)
             def _():
                 for c in d_copies(d + DOWN_SLOTS):
                     c.start()
 
+            @pl.when((j == ATTENTION_AT) & (layer + 1 < layers))
+            def _():
+                start_attention(layer + 1)
+
             @pl.when(j >= LAG)
             def _():
                 combine(j - LAG)
 
             return carry
 
+        down_far(0)
         lax.fori_loop(0, d_chunks, down_body, 0)
-        merge(d_chunks - 1)
+
+        @pl.when(layer + 1 < layers)
+        def _():
+            start_gate_up(layer + 1)
+            start_down(layer + 1)
+
 
         def last_ones(c, carry):
             combine(c)
+
+            @pl.when(layer == layers - 1)
+            def _():
+                relay(c - RELAY_LAG)
+
             return carry
 
         lax.fori_loop(d_chunks - LAG, d_chunks, last_ones, 0)
@@ -417,60 +451,68 @@
         lax.fori_loop(0, d_chunks, sent, 0)
         return carry
 
-    def shift(origin, c, way):
+    def spread_out(origin, c, way, kind=None):
         at = xg.at[origin, :, columns(c)]
-        return remote(at, at, zs.at[way, origin, c], zr.at[origin, c], "pool", p + 1 - 2 * way)
+        return remote(at, at, zs.at[WAYS.index(way) if kind is None else kind, c], zr.at[origin, c], "pool", p + way)
 
     def store(origin, c):
         here = pl.ds(origin * toks, toks)
-        return pltpu.make_async_copy(xg.at[origin, :, columns(c)], out.at[here, columns(c)], osem.at[origin, c])
+        return pltpu.make_async_copy(xg.at[origin, :, columns(c)], out.at[here, columns(c)], osem.at[0])
+
+    def relay(c):
+        @pl.when(p == 1)
+        def _():
+            received(3, c, 2)
+            spread_out(3, c, -1, len(WAYS)).start()
+            store(3, c).start()
+
+        @pl.when(p == 2)
+        def _():
+            received(0, c, -2)
+            spread_out(0, c, 1, len(WAYS)).start()
+            store(0, c).start()
+
+    def received(origin, c, way):
+        spread_out(origin, c, way).wait_recv()
 
     lax.fori_loop(0, layers, layer_body, 0)
 
-    def wave(i, carry):
+    def rest(c, carry):
+        @pl.when(c + RELAY_LAG >= d_chunks)
+        def _():
+            relay(c)
+
         for step in range(1, pools):
-            c = i - (step - 1)
-            live = (c >= 0) & (c < d_chunks)
-
-            @pl.when(live & (p - step >= 0))
-            def _(step=step, c=c):
-                shift(p - step, c, 0).wait_recv()
-
-                @pl.when(p < pools - 1)
-                def _():
-                    shift(p - step, c, 0).start()
-
-                store(p - step, c).start()
-
-            @pl.when(live & (p + step < pools))
-            def _(step=step, c=c):
-                shift(p + step, c, 1).wait_recv()
-
-                @pl.when(p > 0)
-                def _():
-                    shift(p + step, c, 1).start()
-
-                store(p + step, c).start()
+            for origin, way in ((p - step, -1), (p + step, 1)):
+                via_relay = ((p == 1) & (origin == 3)) | ((p == 2) & (origin == 0))
+
+                @pl.when((origin >= 0) & (origin < pools) & jnp.logical_not(via_relay))
+                def _(origin=origin, way=way):
+                    received(origin, c, way)
+                    store(origin, c).start()
 
         return carry
 
-    lax.fori_loop(0, d_chunks + pools - 2, wave, 0)
+    lax.fori_loop(0, d_chunks, rest, 0)
 
     def finish(c, carry):
-        for step in range(pools):
-            @pl.when((p - step >= 0) & (p < pools - 1))
-            def _(step=step):
-                shift(p - step, c, 0).wait_send()
-
-            @pl.when((p + step < pools) & (p > 0))
-            def _(step=step):
-                shift(p + step, c, 1).wait_send()
-
-        for origin in range(pools):
-            store(origin, c).wait()
+        for way in WAYS:
+            @pl.when((p + way >= 0) & (p + way < pools))
+            def _(way=way):
+                spread_out(p, c, way).wait_send()
+
+        @pl.when(p == 1)
+        def _():
+            spread_out(3, c, -1, len(WAYS)).wait_send()
+
+        @pl.when(p == 2)
+        def _():
+            spread_out(0, c, 1, len(WAYS)).wait_send()
+
         return carry
 
     lax.fori_loop(0, d_chunks, finish, 0)
+    pltpu.make_async_copy(out, out, osem.at[0]).wait()
 
 
 def solution(mesh):
@@ -488,9 +530,9 @@
         d_chunks = model // DOWN_COLS
         dma, vmem = pltpu.SemaphoreType.DMA, pltpu.VMEM
         scratch = [
-            vmem((model, heads * head), bf16), vmem((model, 2 * kv_heads * head), bf16), vmem((heads * head, model), bf16),
+            vmem((heads * head, model), bf16),
             vmem((toks, seq * kv_heads, head), bf16), vmem((toks, seq * kv_heads, head), bf16),
-            vmem((GU_SLOTS, 2, model, CHUNK), bf16), vmem((DOWN_SLOTS, local, ff, DOWN_COLS), bf16),
+            vmem((GU_SLOTS, 2, model, GU_COLS), bf16), vmem((DOWN_SLOTS, local, ff, DOWN_COLS), bf16),
             vmem((layers, 4 * toks, model), bf16), vmem((local, 4 * toks, ff), bf16),
             vmem((d_chunks, 4 * toks, DOWN_COLS), f32),
             vmem((layers, d_chunks, toks, DOWN_COLS), f32), vmem((layers, d_chunks, toks, DOWN_COLS), f32),
@@ -502,10 +544,10 @@
             vmem((layers, w_router.shape[2], model), f32),
             vmem(cos_t.shape, f32), vmem(sin_t.shape, f32), vmem((toks, head), f32), vmem((toks, head), f32),
             vmem((layers, 2, toks, LANES), jnp.int32),
-            dma((4,)), dma((KV_BLOCKS, 2)), dma((GU_SLOTS, 2)), dma((DOWN_SLOTS, local)), dma((4,)),
+            dma((3 + heads * head // CHUNK,)), dma((KV_BLOCKS, 2)), dma((GU_SLOTS, 2)), dma((DOWN_SLOTS, local)), dma((4,)),
             dma((3, 2)), dma((layers, 3, 2)), dma((3,)), dma((layers, 3)),
             dma((d_chunks,)), dma((layers, d_chunks)), dma((d_chunks,)), dma((layers, d_chunks)),
-            dma((d_chunks,)), dma((layers, d_chunks)), dma((2, pools, d_chunks)), dma((pools, d_chunks)), dma((pools, d_chunks)),
+            dma((d_chunks,)), dma((layers, d_chunks)), dma((len(WAYS) + 1, d_chunks)), dma((pools, d_chunks)), dma((1,)),
         ]
         smem = pl.BlockSpec(memory_space=pltpu.SMEM)
         anyw = pl.BlockSpec(memory_space=pl.ANY)

time: 113 us -> 104 us (0.920)
  Pallas kernels: 111 us -> 101 us
    pallas_call x1, Pallas kernels: 111 us -> 101 us  [body(): pl.pallas_call(functools.partial(kernel, dims), out_shape=jax.ShapeDtypeS...]
where the time goes in v3:
time: 104 us
  Pallas kernels  101 us (97%)
  local copies, waits for them, and re-layouts  2.06 us (2%)
    pallas_call x1, Pallas kernels, body(): pl.pallas_call(functools.partial(kernel, dims), out_shape=jax.ShapeDtypeS...  101 us

profile of v3, /device:TPU:0, one launch (start us, length us, event | category | flops | bytes accessed | tf_op | source)
XLA Modules:
  0.0 103.5 jit_solution(14182043375106443694)
XLA Ops:
  0.0 101.4 %decode.1 = bf16[256,1536]{1,0:T(8,128)(2,1)} custom-call(s32[256]{0:T(256)} %lens.1, s32[2,2,256]{2,1,0:T(2,128)} %bitcast.7, bf16[256,1536]{1,0:T(8,128)(2,1)} %hid.1, bf16[2,256,256,128]{3,2,1,0:T(8,128)(2,1)} %bitcast.4, bf16[2,256,256,128]{3,2,1,0:T(8,128)(2,1)} %bitcast.5, bf16[2,1536,1536]{2,1,0:T(8,128)(2,1)} %wq.1, bf16[2,1536,256]{2,1,0:T(8,128)(2,1)} %wk.1, ...), custom_call_target="tpu_custom_call" | custom-call | tf_op jit(solution)/shard_map/decode/pallas_call | solution.py:554
  101.5 2.1 %copy.17 = bf16[256,1536]{1,0:T(8,128)(2,1)} copy(bf16[256,1536]{1,0:T(8,128)(2,1)} %decode.1) | data formatting | bytes 1572864

commit v4 on v3

--- a/solution.py
+++ b/solution.py
@@ -23,10 +23,10 @@
 DOWN_COLS = 256
 KV_BLOCKS = 4
 GROUP = 8
-LAG = 4
+LAG = 3
 ATTENTION_AT = 3
 WAYS = (-2, 2, -1, 1)
-RELAY_LAG = 2
+RELAY_LAG = 3
 
 
 def rotary_tables(size):
@@ -42,9 +42,9 @@
     return values * lax.rsqrt(jnp.mean(values * values, axis=-1, keepdims=True) + EPSILON)
 
 
-def kernel(dims, lens, ids, hid, kc, vc, wq, wk, wv, wo, wr, cos_t, sin_t, wg, wu, wd, out,
+def kernel(dims, lens_h, ids_h, hid, kc, vc, wq, wk, wv, wo, wr, cos_t, sin_t, wg, wu, wd, out,
            wo_b, kbuf, vbuf, gu, dbuf, ubuf, inner, stage, part_l, part_m, merged, far, xg, acc_a,
-           q2d, k2d, v2d, o2d, s_even, s_odd, att, gbuf, gsel, wr_b, cosb, sinb, cosr, sinr, id_b,
+           q2d, k2d, v2d, o2d, s_even, s_odd, att, gbuf, gsel, wr_b, lens, ids, cosb, sinb, cosr, sinr, id_b,
            wsem, kvsem, gusem, dsem, isem, us, ur, gs, gr, ps, pr, ms, mr, fs, fr, zs, zr, osem):
     layers, toks, model, ff, heads, local = dims
     e = lax.axis_index("ep")
@@ -127,11 +127,12 @@
     first = [pltpu.make_async_copy(hid.at[pl.ds(start, toks)], acc_a, isem.at[0]),
              pltpu.make_async_copy(wr, wr_b, isem.at[1]),
              pltpu.make_async_copy(cos_t, cosb, isem.at[2]),
-             pltpu.make_async_copy(sin_t, sinb, isem.at[3])]
-    first[0].start()
+             pltpu.make_async_copy(sin_t, sinb, isem.at[3]),
+             pltpu.make_async_copy(lens_h, lens, isem.at[4]),
+             pltpu.make_async_copy(ids_h, ids, isem.at[5])]
+    for c in first:
+        c.start()
     start_projections(0)
-    for c in first[1:]:
-        c.start()
 
     barrier = pltpu.get_barrier_semaphore()
     pl.semaphore_signal(barrier, inc=1, device_id={"ep": partner}, device_id_type=MESH)
@@ -145,6 +146,7 @@
 
     for c in first:
         c.wait()
+    start_caches(0)
 
     zeros = jnp.zeros(((16 - heads) * toks, HEAD), jnp.float32)
     for ref in (q2d, k2d, v2d):
@@ -160,8 +162,7 @@
                 id_b[layer, k, where, :] = jnp.full((1, LANES), ids[layer, k, start + t], jnp.int32)
         return carry
 
-    lax.fori_loop(0, toks, spread, 0)
-    start_caches(0)
+    lax.fori_loop(0, toks, spread, 0, unroll=8)
 
     lane = lax.broadcasted_iota(jnp.int32, (16, seq2), 1)
     head_kv = jnp.where(lax.broadcasted_iota(jnp.int32, (16, seq2), 0) >= group, 1, 0)
@@ -172,19 +173,18 @@
         hidden = acc_a[...].astype(jnp.float32)
         h = normed(hidden).astype(jnp.bfloat16)
         copies = weight_copies(layer)
+        for c in copies[3:] + copies[:2]:
+            c.wait()
         cosine, sine = cosr[...], sinr[...]
 
         def rope(v):
             return (v * cosine + pltpu.roll(v, HEAD // 2, 1) * sine).astype(jnp.bfloat16).astype(jnp.float32)
 
         for n in range(heads * HEAD // CHUNK):
-            copies[3 + n].wait()
             qn = jnp.dot(h, proj(n * CHUNK, CHUNK)[...], preferred_element_type=jnp.float32)
             for k in range(CHUNK // HEAD):
                 head = n * (CHUNK // HEAD) + k
                 q2d[pl.ds(head * toks, toks), :] = rope(qn[:, k * HEAD:(k + 1) * HEAD])
-        copies[0].wait()
-        copies[1].wait()
         kv = jnp.dot(h, proj(q_cols, 2 * kvw)[...], preferred_element_type=jnp.float32)
         for j in range(KV):
             kj = rope(kv[:, j * HEAD:(j + 1) * HEAD])
@@ -244,10 +244,6 @@
 
         lax.fori_loop(0, KV_BLOCKS, attend, 0)
 
-        @pl.when(layer == 0)
-        def _():
-            start_down(0)
-
         for head in range(heads):
             att[:, head * HEAD:(head + 1) * HEAD] = o2d[pl.ds(head * toks, toks), :].astype(jnp.bfloat16)
         copies[2].wait()
@@ -298,43 +294,50 @@
         g_far.start()
         g_near.start()
 
-        def gate_up(low, count, wait, release):
-            def step(i, carry):
-                g = layer * gu_total + i
-                slot = i % GU_SLOTS
-                if wait:
-                    for c in gu_copies(g):
-                        c.wait()
-                for n in range(0, GU_COLS, PIECE):
-                    tokens = ubuf[layer, low:low + count, :]
-                    one = jnp.dot(tokens, gu[slot, 0, :, n:n + PIECE], preferred_element_type=jnp.float32)
-                    three = jnp.dot(tokens, gu[slot, 1, :, n:n + PIECE], preferred_element_type=jnp.float32)
-                    cols = pl.ds(pl.multiple_of((i % ff_chunks) * GU_COLS + n, PIECE), PIECE)
-                    inner[i // ff_chunks, low:low + count, cols] = (jax.nn.silu(one) * three).astype(jnp.bfloat16)
-                if release:
-                    @pl.when(i + GU_SLOTS < gu_total)
-                    def _():
-                        for c in gu_copies(g + GU_SLOTS):
-                            c.start()
-
-                return carry
-
-            return step
+        def rows_of(i, low, count):
+            slot = i % GU_SLOTS
+            for n in range(0, GU_COLS, PIECE):
+                tokens = ubuf[layer, low:low + count, :]
+                one = jnp.dot(tokens, gu[slot, 0, :, n:n + PIECE], preferred_element_type=jnp.float32)
+                three = jnp.dot(tokens, gu[slot, 1, :, n:n + PIECE], preferred_element_type=jnp.float32)
+                cols = pl.ds(pl.multiple_of((i % ff_chunks) * GU_COLS + n, PIECE), PIECE)
+                inner[i // ff_chunks, low:low + count, cols] = (jax.nn.silu(one) * three).astype(jnp.bfloat16)
+
+        def near_step(i, carry):
+            for c in gu_copies(layer * gu_total + i):
+                c.wait()
+            rows_of(i, 0, 2 * toks)
+            return carry
+
+        def far_step(m, carry):
+            for i in (2 * m, 2 * m + 1):
+                rows_of(i, 2 * toks, 2 * toks)
+                for c in gu_copies(layer * gu_total + i + GU_SLOTS):
+                    c.start()
+            return carry
+
+        def all_step(i, carry):
+            for c in gu_copies(layer * gu_total + i):
+                c.wait()
+            rows_of(i, 0, 4 * toks)
+            return carry
 
         for c in u_near:
             c.wait_recv()
-        lax.fori_loop(0, 2, gate_up(0, 2 * toks, True, False), 0)
-        u_far[0].wait_recv()
-        u_pass[0].start()
-        lax.fori_loop(2, GU_SLOTS, gate_up(0, 2 * toks, True, False), 0)
-        u_far[1].wait_recv()
-        u_pass[1].start()
+        lax.fori_loop(0, GU_SLOTS, near_step, 0)
+        for h in range(2):
+            u_far[h].wait_recv()
+            u_pass[h].start()
         g_far.wait_recv()
         g_pass.start()
         for c in u_pass:
             c.wait_recv()
-        lax.fori_loop(0, GU_SLOTS, gate_up(2 * toks, 2 * toks, False, True), 0)
-        lax.fori_loop(GU_SLOTS, gu_total, gate_up(0, 4 * toks, True, True), 0)
+        lax.fori_loop(0, GU_SLOTS // 2, far_step, 0)
+        @pl.when(layer == 0)
+        def _():
+            start_down(0)
+
+        lax.fori_loop(GU_SLOTS, gu_total, all_step, 0)
 
         g_near.wait_recv()
         g_pass.wait_recv()
@@ -367,7 +370,7 @@
 
             @pl.when(layer == layers - 1)
             def _():
-                xg[p, :, columns(c)] = x
+                xg[p, c] = x
                 store(p, c).start()
 
                 for way in WAYS:
@@ -387,20 +390,18 @@
             for n in range(len(terms)):
                 stage[j, low:low + 2 * toks, n * LANES:(n + 1) * LANES] = terms[n]
 
-        def down_far(j):
-            for c in d_copies(layer * d_chunks + j):
+        def down_body(j, carry):
+            d = layer * d_chunks + j
+
+            for c in d_copies(d):
                 c.wait()
             down(j, j % DOWN_SLOTS, 2 * toks)
             near_m(j).start()
 
-        def down_body(j, carry):
-            d = layer * d_chunks + j
-
-            @pl.when(j + 1 < d_chunks)
-            def _():
-                down_far(j + 1)
-
-            merge(j)
+            @pl.when(j > 0)
+            def _():
+                merge(j - 1)
+
             down(j, j % DOWN_SLOTS, 0)
             near_l(j).start()
 
@@ -413,14 +414,14 @@
             def _():
                 start_attention(layer + 1)
 
-            @pl.when(j >= LAG)
+            @pl.when((j >= LAG) & (layer == layers - 1))
             def _():
                 combine(j - LAG)
 
             return carry
 
-        down_far(0)
         lax.fori_loop(0, d_chunks, down_body, 0)
+        merge(d_chunks - 1)
 
         @pl.when(layer + 1 < layers)
         def _():
@@ -437,7 +438,7 @@
 
             return carry
 
-        lax.fori_loop(d_chunks - LAG, d_chunks, last_ones, 0)
+        lax.fori_loop((d_chunks - LAG) * (layer // (layers - 1)), d_chunks, last_ones, 0)
 
         for c in u_near + u_far + u_pass + [g_near, g_far, g_pass]:
             c.wait_send()
@@ -452,12 +453,12 @@
         return carry
 
     def spread_out(origin, c, way, kind=None):
-        at = xg.at[origin, :, columns(c)]
+        at = xg.at[origin, c]
         return remote(at, at, zs.at[WAYS.index(way) if kind is None else kind, c], zr.at[origin, c], "pool", p + way)
 
     def store(origin, c):
         here = pl.ds(origin * toks, toks)
-        return pltpu.make_async_copy(xg.at[origin, :, columns(c)], out.at[here, columns(c)], osem.at[0])
+        return pltpu.make_async_copy(xg.at[origin, c], out.at[here, columns(c)], osem.at[0])
 
     def relay(c):
         @pl.when(p == 1)
@@ -478,10 +479,6 @@
     lax.fori_loop(0, layers, layer_body, 0)
 
     def rest(c, carry):
-        @pl.when(c + RELAY_LAG >= d_chunks)
-        def _():
-            relay(c)
-
         for step in range(1, pools):
             for origin, way in ((p - step, -1), (p + step, 1)):
                 via_relay = ((p == 1) & (origin == 3)) | ((p == 2) & (origin == 0))
@@ -493,6 +490,11 @@
 
         return carry
 
+    def last_relays(c, carry):
+        relay(c)
+        return carry
+
+    lax.fori_loop(d_chunks - RELAY_LAG, d_chunks, last_relays, 0)
     lax.fori_loop(0, d_chunks, rest, 0)
 
     def finish(c, carry):
@@ -537,24 +539,24 @@
             vmem((d_chunks, 4 * toks, DOWN_COLS), f32),
             vmem((layers, d_chunks, toks, DOWN_COLS), f32), vmem((layers, d_chunks, toks, DOWN_COLS), f32),
             vmem((d_chunks, toks, DOWN_COLS), f32), vmem((layers, d_chunks, toks, DOWN_COLS), f32),
-            vmem((pools, toks, model), bf16), vmem((toks, model), bf16),
+            vmem((pools, d_chunks, toks, DOWN_COLS), bf16), vmem((toks, model), bf16),
             vmem((16 * toks, head), f32), vmem((16 * toks, head), f32), vmem((16 * toks, head), f32), vmem((16 * toks, head), f32),
             vmem((GROUP * 16, seq * kv_heads), f32), vmem((GROUP * 16, seq * kv_heads), f32),
             vmem((toks, heads * head), bf16), vmem((layers, 4 * toks, LANES), f32), vmem((local, 4 * toks, LANES), f32),
             vmem((layers, w_router.shape[2], model), f32),
+            pltpu.SMEM((shard,), jnp.int32), pltpu.SMEM((layers, 2, shard), jnp.int32),
             vmem(cos_t.shape, f32), vmem(sin_t.shape, f32), vmem((toks, head), f32), vmem((toks, head), f32),
             vmem((layers, 2, toks, LANES), jnp.int32),
-            dma((3 + heads * head // CHUNK,)), dma((KV_BLOCKS, 2)), dma((GU_SLOTS, 2)), dma((DOWN_SLOTS, local)), dma((4,)),
+            dma((3 + heads * head // CHUNK,)), dma((KV_BLOCKS, 2)), dma((GU_SLOTS, 2)), dma((DOWN_SLOTS, local)), dma((6,)),
             dma((3, 2)), dma((layers, 3, 2)), dma((3,)), dma((layers, 3)),
             dma((d_chunks,)), dma((layers, d_chunks)), dma((d_chunks,)), dma((layers, d_chunks)),
             dma((d_chunks,)), dma((layers, d_chunks)), dma((len(WAYS) + 1, d_chunks)), dma((pools, d_chunks)), dma((1,)),
         ]
-        smem = pl.BlockSpec(memory_space=pltpu.SMEM)
         anyw = pl.BlockSpec(memory_space=pl.ANY)
         return pl.pallas_call(
             functools.partial(kernel, dims),
             out_shape=jax.ShapeDtypeStruct((shard, model), bf16),
-            in_specs=[smem, smem] + [anyw] * 13,
+            in_specs=[anyw] * 15,
             out_specs=anyw,
             scratch_shapes=scratch,
             compiler_params=pltpu.CompilerParams(collective_id=0, has_side_effects=True, vmem_limit_bytes=67043328),

time: 104 us -> 94.8 us (0.912)
  Pallas kernels: 101 us -> 92.6 us
    pallas_call x1, Pallas kernels: 101 us -> 92.6 us  [body(): pl.pallas_call(functools.partial(kernel, dims), out_shape=jax.ShapeDtypeS...]
where the time goes in v4:
time: 94.8 us; the launch traced here: 94.6 us
  Pallas kernels  92.6 us (98%)
  local copies, waits for them, and re-layouts  2.06 us (2%)
    pallas_call x1, Pallas kernels, body(): pl.pallas_call(functools.partial(kernel, dims), out_shape=jax.ShapeDtypeS...  92.6 us
    unnamed x1, local copies, waits for them, and re-layouts  2.06 us

profile of v4, /device:TPU:0, one launch (start us, length us, event | category | flops | bytes accessed | tf_op | source)
XLA Modules:
  0.0 94.6 jit_solution(7375765257086902995)
XLA Ops:
  0.0 92.6 %decode.1 = bf16[256,1536]{1,0:T(8,128)(2,1)} custom-call(s32[256]{0:T(256)} %lens_h.1, s32[2,2,256]{2,1,0:T(2,128)} %bitcast.7, bf16[256,1536]{1,0:T(8,128)(2,1)} %hid.1, bf16[2,256,256,128]{3,2,1,0:T(8,128)(2,1)} %bitcast.4, bf16[2,256,256,128]{3,2,1,0:T(8,128)(2,1)} %bitcast.5, bf16[2,1536,1536]{2,1,0:T(8,128)(2,1)} %wq.1, bf16[2,1536,256]{2,1,0:T(8,128)(2,1)} %wk.1, ...), custom_call_target="tpu_custom_call" | custom-call | tf_op jit(solution)/shard_map/decode/pallas_call | solution.py:556
  92.6 2.1 %copy.17 = bf16[256,1536]{1,0:T(8,128)(2,1)} copy(bf16[256,1536]{1,0:T(8,128)(2,1)} %decode.1) | data formatting | bytes 1572864
